TPU v7x, 128 devices: a whole 4x4x4 slice. The times are simulated.
128 devices in a mesh: vocab: 8 (over x, core), expert: 16 (over y, z).
Axes of the slice: x: 4, y: 4, z: 4, core: 2. Of those that a mesh axis runs over, the one named last changes fastest.
Arguments:
- leading_batch_features: bfloat16 [1024, 2880], P(('vocab', 'expert')), may hold values from -48 to 48
- sampling_heat_selector: int32 [1024], replicated, may hold values from 0 to 3
- output_embedding_matrix: bfloat16 [201088, 2880], P(('vocab', 'expert')), may hold values from -3.354102 to 3.354102
- trailing_batch_features: bfloat16 [1024, 2880], P('expert'), may hold values from -6 to 6
- routed_specialist_choice: int32 [1024, 4], P('expert'), may hold values from 0 to 63, all different within a row; in each aligned block of 64 rows (0 to 63, 64 to 127, ...) at most 8 rows name the same one
- dispatcher_projection: bfloat16 [2880, 64], replicated, may hold values from -13.416408 to 13.416408
- specialist_gating_matrix: bfloat16 [64, 2880, 1440], P('expert', None, 'vocab'), may hold values from -0.109375 to 0.109375
- specialist_raising_matrix: bfloat16 [64, 2880, 1440], P('expert', None, 'vocab'), may hold values from -0.109375 to 0.109375
- expert_lowering_matrix: bfloat16 [64, 1440, 2880], P('expert', 'vocab'), may hold values from -0.15625 to 0.15625
Outputs:
- lexicon_log_probability: float32 [1024, 201088], P(None, ('vocab', 'expert'))
- moe_out: bfloat16 [1024, 2880], P('expert', 'vocab')
Inputs may be any that keep to these rules, and one draw needn't show every extreme that they name: `routed_specialist_choice`: in the rows of one index of the expert axis no expert is named more than 8 times, a bound that some block reaches.
All inputs are finite; a program needn't handle non-finite values.
Results may differ from a plain program's by a relative error of at most 0.005.
The roundings to bfloat16 on the way count: a program that leaves them out, or rounds other values in their place, can miss the bound.
Values may be sent and summed in bfloat16 or wider, within the bound.
A program may use at most 256 MiB of HBM per device.

v0:
```python
import jax
import jax.numpy as jnp
from jax import lax
from jax.sharding import Mesh
from jax.sharding import PartitionSpec as P

VOCAB_EXPERT = ("vocab_0", "vocab_1", "expert_0", "expert_1")
EXPERT = ("expert_0", "expert_1")
VOCAB = ("vocab_0", "vocab_1")


def gathered_once(x, axis):
    leaves = jax.tree.leaves(x)
    turns = sorted(range(len(leaves)), key=lambda k: -leaves[k].size)
    width = (1, *leaves[turns[0]].shape)[-1]
    lines = [
        jnp.pad(leaves[k].reshape(-1), (0, -leaves[k].size % width)).reshape(-1, width)
        for k in turns
    ]
    both, at, found = (lax.all_gather(jnp.concatenate(lines), axis), 0, {})
    for k, line in zip(turns, lines):
        share = both[:, at : at + len(line)].reshape(len(both), -1)
        found[k] = share[:, : leaves[k].size].reshape(-1, *leaves[k].shape)
        at += len(line)
    numbers = iter(range(len(leaves)))
    return jax.tree.map(lambda _: found[next(numbers)], x)


def merged_by_axis(x, axes, combine):
    for axis in axes:
        pieces = gathered_once(x, axis)
        x = jax.tree.map(lambda part: part[0], pieces)
        for k in range(1, lax.axis_size(axis)):
            x = combine(x, jax.tree.map(lambda part: part[k], pieces))
    return x


def cut_along(x, dim, devices):
    lengths = x.shape
    parts = x.reshape(*lengths[:dim], devices, lengths[dim] // devices, *lengths[dim + 1 :])
    return jnp.moveaxis(parts, dim, 0)


def sent_and_summed(x, axis, dim):
    devices = lax.axis_size(axis)
    parts = lax.all_to_all(cut_along(x, dim, devices), axis, 0, 0, tiled=True)
    return jnp.sum(parts, axis=0)


def slot_numbers(flat_ids, expert_count):
    one_hot = (flat_ids[:, None] == jnp.arange(expert_count, dtype=jnp.int32)[None, :]).astype(
        jnp.int32
    )
    earlier = jnp.cumsum(one_hot, axis=0) - one_hot
    return jnp.sum(earlier * one_hot, axis=1)


def pair_join(first, second):
    largest = jnp.maximum(first[0], second[0])
    return (
        largest,
        first[1] * jnp.exp(first[0] - largest) + second[1] * jnp.exp(second[0] - largest),
    )


def per_device(
    leading_batch_features,
    sampling_heat_selector,
    output_embedding_matrix,
    trailing_batch_features,
    routed_specialist_choice,
    dispatcher_projection,
    specialist_gating_matrix,
    specialist_raising_matrix,
    expert_lowering_matrix,
):
    position_heat_factor = 0.5 + 0.25 * sampling_heat_selector.astype(jnp.float32)
    plain_lexicon_scores = lax.dot_general(
        lax.all_gather(leading_batch_features, VOCAB_EXPERT, axis=0, tiled=True),
        output_embedding_matrix,
        (((1,), (1,)), ((), ())),
        preferred_element_type=jnp.float32,
    )
    heat_divided_scores = plain_lexicon_scores / position_heat_factor[:, None]
    local_max = jnp.max(heat_divided_scores, axis=1)
    local_total = jnp.sum(jnp.exp(heat_divided_scores - local_max[:, None]), axis=1)
    row_max, row_total = merged_by_axis((local_max, local_total), VOCAB_EXPERT, pair_join)
    lexicon_log_probability = heat_divided_scores - row_max[:, None] - jnp.log(row_total)[:, None]
    tok_count = trailing_batch_features.shape[0]
    width_full = trailing_batch_features.shape[1]
    top_count = routed_specialist_choice.shape[1]
    expert_count = dispatcher_projection.shape[1]
    local_experts = specialist_gating_matrix.shape[0]
    expert_devices = lax.axis_size(EXPERT)
    capacity = max(2, 2 * top_count * tok_count // expert_count)
    router_full = jnp.dot(
        trailing_batch_features, dispatcher_projection, preferred_element_type=jnp.float32
    )
    scores = jnp.take_along_axis(router_full, routed_specialist_choice, axis=1)
    gate_probs = jax.nn.softmax(scores, axis=1)
    slots = slot_numbers(routed_specialist_choice.reshape(-1), expert_count)
    slot_index = routed_specialist_choice.reshape(-1) * capacity + slots
    token_rows = jnp.repeat(trailing_batch_features, top_count, axis=0)
    outgoing = (
        jnp.zeros((expert_count * capacity, width_full), jnp.bfloat16)
        .at[slot_index]
        .set(token_rows)
    )
    outgoing = outgoing.reshape(expert_devices, local_experts, capacity, width_full)
    received = lax.all_to_all(outgoing, EXPERT, split_axis=0, concat_axis=0, tiled=True)
    gate_proj = jnp.einsum(
        "secd,edf->secf", received, specialist_gating_matrix, preferred_element_type=jnp.float32
    )
    up_proj = jnp.einsum(
        "secd,edf->secf", received, specialist_raising_matrix, preferred_element_type=jnp.float32
    )
    activated = (gate_proj * jax.nn.sigmoid(1.702 * gate_proj) * (up_proj + 1.0)).astype(
        jnp.bfloat16
    )
    partial_value = jnp.einsum(
        "secf,efd->secd", activated, expert_lowering_matrix, preferred_element_type=jnp.float32
    )
    shares = sent_and_summed(partial_value, VOCAB, 3).astype(jnp.bfloat16)
    returned = lax.all_to_all(shares, EXPERT, split_axis=0, concat_axis=0, tiled=True)
    returned = returned.reshape(expert_count * capacity, returned.shape[3])
    picked = (
        returned[slot_index].reshape(tok_count, top_count, returned.shape[1]).astype(jnp.float32)
    )
    moe_out = jnp.sum(gate_probs[:, :, None] * picked, axis=1).astype(jnp.bfloat16)
    return (lexicon_log_probability, moe_out)


def solution(mesh):
    torus = Mesh(mesh.devices.reshape(4, 2, 4, 4), ("vocab_0", "vocab_1", "expert_0", "expert_1"))
    placed = (
        P(VOCAB_EXPERT, None),
        P(),
        P(VOCAB_EXPERT, None),
        P(EXPERT, None),
        P(EXPERT, None),
        P(),
        P(EXPERT, None, VOCAB),
        P(EXPERT, None, VOCAB),
        P(EXPERT, VOCAB, None),
    )
    return jax.shard_map(
        per_device,
        mesh=torus,
        in_specs=placed,
        out_specs=(P(None, VOCAB_EXPERT), P(EXPERT, VOCAB)),
        check_vma=False,
    )
```

profile of v0, /device:TPU:0, one launch (start us, length us, event | category | flops | bytes accessed | tf_op | source)
XLA Modules:
  0.0 253.6 jit_solution(7647103900642919661)
XLA Ops:
  7.2 0.0 copy-start
  7.2 0.0 all-gather.10.cloned.1.call-start
  7.2 0.7 all-gather.10.cloned.1.call-update
  7.9 0.8 copy.64
  8.7 0.1 eq.29
  8.8 0.1 eq.25
  8.9 0.6 reduce-window.6
  9.5 0.2 slice_reduce_fusion
  9.8 0.7 broadcast_multiply_fusion
  10.5 0.1 copy.63
  10.6 0.1 mul.252
  10.7 1.4 broadcast_in_dim.10
  12.0 1.6 reshape.688
  13.7 0.1 fusion.36
  13.8 4.6 %scatter_custom_fusion = bf16[512,2880]{1,0:T(8,128)(2,1)S(1)} fusion(s32[256]{0:T(256)S(1)} %bitcast.260, bf16[256,2880]{1,0:T(8,128)(2,1)} %reshape.688, bf16[]{:T(256)} %constant.12.clone.1), kind=kCustom, calls=%fused_computation.15 | custom fusion | bytes 2949632 | tf_op jit(solution)/shard_map/scatter | solution.py:107
  18.3 48.3 %all_to_all.15 = bf16[16,4,8,2880]{3,2,1,0:T(8,128)(2,1)S(1)} all-to-all(bf16[16,4,8,2880]{3,2,1,0:T(8,128)(2,1)S(1)} %bitcast.241), channel_id=1, replica_groups=mesh['vocab_0'=4,'vocab_1'=2,'expert_0'=4,'expert_1'=4] {'expert_0','exp..., dimensions={0} | all-to-all | bytes 5898240 | tf_op jit(solution)/shard_map/all_to_all | solution.py:110
  66.6 3.9 %fusion.9 = f32[16,4,8,180]{3,2,0,1:T(8,128)S(1)} fusion(bf16[4,2880,180,1]{1,0,2,3:T(4,128)(2,1)} %bitcast.262, bf16[16,4,8,2880]{3,2,1,0:T(8,128)(2,1)S(1)} %all_to_all.15), kind=kOutput, calls=%fused_computation.17 | convolution fusion | flops 530841600 | bytes 7464960 | tf_op jit(solution)/shard_map/secd,edf->secf/dot_general | solution.py:111
  70.5 0.0 slice-start.1
  70.5 3.8 %fusion.29 = bf16[16,4,8,180]{3,2,0,1:T(8,128)(2,1)S(1)} fusion(bf16[4,2880,180,1]{1,0,2,3:T(4,128)(2,1)} %bitcast.263, bf16[16,4,8,2880]{3,2,1,0:T(8,128)(2,1)S(1)} %all_to_all.15, f32[16,4,8,180]{3,2,0,1:T(8,128)S(1)} %fusion.9), kind=kOutput, calls=%fused_computation.21 | convolution fusion | flops 531578880 | bytes 7649280 | tf_op jit(solution)/shard_map/secd,edf->secf/dot_general | solution.py:114
  74.3 3.6 %convolution_bitcast_fusion = f32[16,4,8,2880]{3,2,0,1:T(8,128)} fusion(bf16[16,4,8,180]{3,2,0,1:T(8,128)(2,1)S(1)} %fusion.29, bf16[4,180,2880,1]{2,0,1,3:T(4,128)(2,1)S(1)} %bitcast.245), kind=kOutput, calls=%fused_computation.6 | convolution fusion | flops 530841600 | bytes 10229760 | tf_op jit(solution)/shard_map/secf,efd->secd/dot_general | solution.py:120
  78.0 8.3 %reshape.667 = f32[16,4,8,8,360]{4,3,2,0,1:T(8,128)} reshape(f32[16,4,8,2880]{3,2,0,1:T(8,128)} %convolution_bitcast_fusion) | data formatting | bytes 11796480 | tf_op jit(solution)/shard_map/reshape | solution.py:40
  86.3 6.7 %copy.118 = f32[16,4,8,8,360]{4,2,0,1,3:T(8,128)} copy(f32[16,4,8,8,360]{4,3,2,0,1:T(8,128)} %reshape.667) | data formatting | bytes 11796480 | tf_op jit(solution)/shard_map/reshape | solution.py:40
  93.0 5.0 %all-to-all-start.1 = ((f32[8,16,4,8,360]{4,3,1,2,0:T(8,128)}), f32[8,16,4,8,360]{4,3,1,2,0:T(8,128)}, u32[]{:S(2)}, u32[]{:S(2)}) async-start(f32[8,16,4,8,360]{4,3,1,2,0:T(8,128)} %bitcast.240), calls=%async_computation.1 | async-start | bytes 12582912 | tf_op jit(solution)/shard_map/all_to_all | solution.py:46
  98.0 0.1 copy.60
  98.1 0.1 reshape.678
  98.3 0.3 fusion.75
  98.5 1.9 gather_fusion.1
  100.5 0.0 copy-start.4
  100.5 0.1 reshape.681
  100.6 0.1 copy.61
  100.7 69.2 %all-to-all-done.1 = f32[8,16,4,8,360]{4,3,1,2,0:T(8,128)} async-done(((f32[8,16,4,8,360]{4,3,1,2,0:T(8,128)}), f32[8,16,4,8,360]{4,3,1,2,0:T(8,128)}, u32[]{:S(2)}, u32[]{:S(2)}) %all-to-all-start.1) | async-done | bytes 5898272 | tf_op jit(solution)/shard_map/all_to_all | solution.py:46
  169.9 3.3 %reduce_sum.51 = bf16[16,4,8,360]{3,2,0,1:T(8,128)(2,1)S(1)} reduce(f32[8,16,4,8,360]{4,3,1,2,0:T(8,128)} %all-to-all-done.1, f32[]{:T(128)} %constant.16.clone.1), dimensions={0}, to_apply=%region_8.9 | reduce | flops 1290240 | bytes 6266884 | tf_op jit(solution)/shard_map/reduce_sum | solution.py:47
  173.2 0.8 copy.74
  174.0 3.9 %all-to-all-start.2 = ((bf16[16,4,8,360]{3,2,1,0:T(8,128)(2,1)}), bf16[16,4,8,360]{3,2,1,0:T(8,128)(2,1)S(1)}, u32[]{:S(2)}, u32[]{:S(2)}) async-start(bf16[16,4,8,360]{3,2,1,0:T(8,128)(2,1)} %copy.74), calls=%async_computation.2 | async-start | bytes 786432 | tf_op jit(solution)/shard_map/all_to_all | solution.py:124
  177.9 0.1 copy.62
  178.0 9.4 %all-to-all-done.2 = bf16[16,4,8,360]{3,2,1,0:T(8,128)(2,1)S(1)} async-done(((bf16[16,4,8,360]{3,2,1,0:T(8,128)(2,1)}), bf16[16,4,8,360]{3,2,1,0:T(8,128)(2,1)S(1)}, u32[]{:S(2)}, u32[]{:S(2)}) %all-to-all-start.2) | async-done | bytes 368672 | tf_op jit(solution)/shard_map/all_to_all | solution.py:124
  187.4 1.2 gather_fusion
  188.6 0.1 reshape.669
  188.7 0.9 multiply_reduce_fusion
  189.7 14.7 %fusion.74 = (f32[1024]{0:T(1024)S(1)}, f32[1024,1571]{0,1:T(8,128)S(1)}) fusion(f32[1024]{0:T(1024)S(1)} %multiply_add_fusion, bf16[1024,2880]{1,0:T(8,128)(2,1)} %all-gather.10.cloned.1.call-done, bf16[1571,2880]{1,0:T(8,128)(2,1)} %param.11), kind=kOutput, calls=%fused_computation.98 | convolution fusion | flops 9269351424 | bytes 21390208 | tf_op jit(solution)/shard_map/dot_general | solution.py:78
  204.3 1.0 exponential_reduce_fusion
  205.3 11.9 %all-gather.4 = f32[4,2,1024]{2,1,0:T(2,128)S(1)} all-gather(f32[1,2,1024]{2,1,0:T(2,128)S(1)} %maximum_bitcast_fusion), channel_id=2, replica_groups=mesh['vocab_0'=4,'vocab_1'=2,'expert_0'=4,'expert_1'=4] {'vocab_0'}, dimensions={0}, use_global_device_ids=true | all-gather | bytes 40960 | tf_op jit(solution)/shard_map/all_gather | solution.py:20
  217.2 0.1 fusion.51
  217.3 1.8 all-gather.5
  219.2 11.9 %all-gather.6 = f32[4,2,1024]{2,1,0:T(2,128)S(1)} all-gather(f32[1,2,1024]{2,1,0:T(2,128)S(1)} %maximum_bitcast_fusion.2), channel_id=4, replica_groups=mesh['vocab_0'=4,'vocab_1'=2,'expert_0'=4,'expert_1'=4] {'expert_0'}, dimensions={0}, use_global_device_ids=true | all-gather | bytes 40960 | tf_op jit(solution)/shard_map/all_gather | solution.py:20
  231.1 0.1 fusion.39
  231.2 11.9 %all-gather.7 = f32[4,2,1024]{2,1,0:T(2,128)S(1)} all-gather(f32[1,2,1024]{2,1,0:T(2,128)S(1)} %maximum_bitcast_fusion.3), channel_id=5, replica_groups=mesh['vocab_0'=4,'vocab_1'=2,'expert_0'=4,'expert_1'=4] {'expert_1'}, dimensions={0}, use_global_device_ids=true | all-gather | bytes 40960 | tf_op jit(solution)/shard_map/all_gather | solution.py:20
  243.2 3.6 %subtract_subtract_fusion = f32[1024,1571]{0,1:T(8,128)} fusion(f32[1024,1571]{0,1:T(8,128)S(1)} %get-tuple-element.23, f32[1024]{0:T(1024)S(1)} %get-tuple-element.4, f32[1024]{0:T(1024)S(1)} %get-tuple-element.5), kind=kLoop, calls=%fused_computation.3 | loop fusion | flops 3217408 | bytes 12877824 | tf_op jit(solution)/shard_map/sub | solution.py:88
  (31 shorter events, 0.3 us)
Async XLA Ops:
  7.2 91.1 %copy-start = (bf16[2880,64]{0,1:T(8,128)(2,1)S(1)}, bf16[2880,64]{0,1:T(8,128)(2,1)}, u32[]{:S(2)}) copy-start(bf16[2880,64]{0,1:T(8,128)(2,1)} %param.14) | copy-start | bytes 1105924
  7.2 182.5 %all-gather.10.cloned.1.call-start = ((), (), s32[]{:S(2)}) async-start(), calls=%async_computation.3 | async-start | bytes 6076416 | tf_op jit(solution)/shard_map/all_gather | solution.py:79
  66.6 7.7 %slice-start = ((s8[4239360]{0:T(1024)(128)(4,1)}), s8[4194304]{0:T(1024)(128)(4,1)S(1)}, s32[]{:S(2)}) async-start(s8[4239360]{0:T(1024)(128)(4,1)} %bitcast.243), calls=%async_computation.4 | async-start | bytes 8388608
  70.5 3.8 %slice-start.1 = ((s8[4239360]{0:T(1024)(128)(4,1)}), s8[45056]{0:T(1024)(128)(4,1)S(1)}, s32[]{:S(2)}) async-start(s8[4239360]{0:T(1024)(128)(4,1)} %bitcast.243), calls=%async_computation.5 | async-start | bytes 90112
  92.9 5.1 %copy-start.3 = (s32[64,4]{0,1:T(4,128)S(1)}, s32[64,4]{0,1:T(4,128)}, u32[]{:S(2)}) copy-start(s32[64,4]{0,1:T(4,128)} %param.13) | copy-start | bytes 3076
  93.0 5.3 %copy-start.2 = (bf16[64,2880]{1,0:T(8,128)(2,1)S(1)}, bf16[64,2880]{1,0:T(8,128)(2,1)}, u32[]{:S(2)}) copy-start(bf16[64,2880]{1,0:T(8,128)(2,1)} %param.12) | copy-start | bytes 1105924
  93.0 77.0 %all-to-all-start.1 = ((f32[8,16,4,8,360]{4,3,1,2,0:T(8,128)}), f32[8,16,4,8,360]{4,3,1,2,0:T(8,128)}, u32[]{:S(2)}, u32[]{:S(2)}) async-start(f32[8,16,4,8,360]{4,3,1,2,0:T(8,128)} %bitcast.240), calls=%async_computation.1 | async-start | bytes 12582912 | tf_op jit(solution)/shard_map/all_to_all | solution.py:46
  100.5 77.5 %copy-start.4 = (s32[1024]{0:T(1024)S(1)}, s32[1024]{0:T(1024)}, u32[]{:S(2)}) copy-start(s32[1024]{0:T(1024)} %param.10) | copy-start | bytes 12292
  174.0 13.4 %all-to-all-start.2 = ((bf16[16,4,8,360]{3,2,1,0:T(8,128)(2,1)}), bf16[16,4,8,360]{3,2,1,0:T(8,128)(2,1)S(1)}, u32[]{:S(2)}, u32[]{:S(2)}) async-start(bf16[16,4,8,360]{3,2,1,0:T(8,128)(2,1)} %copy.74), calls=%async_computation.2 | async-start | bytes 786432 | tf_op jit(solution)/shard_map/all_to_all | solution.py:124
  243.2 3.6 %copy-start.1 = (bf16[2880,64]{0,1:T(8,128)(2,1)S(1)}, bf16[2880,64]{0,1:T(8,128)(2,1)}, u32[]{:S(2)}) copy-start(bf16[2880,64]{0,1:T(8,128)(2,1)} %param.14) | copy-start | bytes 1105924
Sparse Core Ops, SparseCore 0:
  11.0 80.3 all-gather.9
where the time goes:
time: 254 us
  blocking collectives  85.9 us (34%)
  waiting for transfers between devices  79.3 us (31%)
  local copies, waits for them, and re-layouts  28.4 us (11%)
  matrix products  26.2 us (10%)
  between operations  14.3 us (6%)
  other arithmetic  10.5 us (4%)
  starting transfers between devices  9 us (4%)
    all_to_all x1, waiting for transfers between devices, sent_and_summed(): parts = lax.all_to_all(cut_along(x, dim, devices), axis, 0, 0, tiled=True)  69.2 us
    all_to_all x1, blocking collectives, per_device(): lax.all_to_all(outgoing, EXPERT, split_axis=0, concat_axis=0, tiled=True)  48.3 us
    all_gather x4, blocking collectives, gathered_once(): both, at, found = (lax.all_gather(jnp.concatenate(lines), axis), 0, {})  37.6 us
    reshape x2, local copies, waits for them, and re-layouts, cut_along(): x.reshape(*lengths[:dim], devices, lengths[dim] // devices, *lengths[dim...  15 us
    dot_general x1, matrix products, per_device(): lax.dot_general(lax.all_gather(leading_batch_features, VOCAB_EXPERT, axis...  14.7 us
    all_to_all x1, waiting for transfers between devices, per_device(): lax.all_to_all(shares, EXPERT, split_axis=0, concat_axis=0, tiled=True)  9.39 us
  transfers between devices with their start and end apart: 3, of which 2 were waited for; matrix products, arithmetic and copies ran while one was open for 18% of the time, Pallas kernels for 0%

commit v1 on v0

v1 whole, which is shorter than its diff:
```python
import functools

import jax
import jax.numpy as jnp
from jax import lax
from jax.experimental import pallas as pl
from jax.experimental.pallas import tpu as pltpu
from jax.sharding import Mesh
from jax.sharding import PartitionSpec as P

AXES = ("x", "c", "y", "z")
EXPERT = ("y", "z")
VOCAB = ("x", "c")
MESH = pl.DeviceIdType.MESH
COLS = ((0, 1024), (1024, 1024), (2048, 832))
ORDERS = (("z", "y", "x"), ("x", "z", "y"), ("y", "x", "z"))
EX, HOLD, SLOTS = 64, 4, 8


def ring(me, axis, step):
    return {axis: lax.rem(me[axis] + step, 4)}


def greet():
    me = {a: lax.axis_index(a) for a in AXES}
    barrier = pltpu.get_barrier_semaphore()
    for a in ("x", "y", "z"):
        for k in range(1, 4):
            pl.semaphore_signal(barrier, inc=1, device_id=ring(me, a, k), device_id_type=MESH)
    pl.semaphore_signal(barrier, inc=1, device_id={"c": 1 - me["c"]}, device_id_type=MESH)
    pl.semaphore_wait(barrier, 10)
    return me


def view(g, me, ranges, cols, at={}):
    idx = [ranges.get(a, at.get(a, me[a])) for a in AXES]
    return g.at[idx[0], idx[1], idx[2], idx[3], :, pl.ds(*cols)]


def remote(src, dst, ssem, rsem, dev, sends):
    cp = pltpu.make_async_remote_copy(
        src_ref=src, dst_ref=dst, send_sem=ssem, recv_sem=rsem, device_id=dev, device_id_type=MESH
    )
    cp.start()
    sends.append(cp)
    return cp


ALL = pl.ds(0, 4)


class Gather:
    def __init__(self, a, g, me, ssem, rsem, own):
        self.a, self.g, self.me, self.ssem, self.rsem = a, g, me, ssem, rsem
        self.sends, self.mates, self.got = [], [], [None] * 3
        self.own = pltpu.make_async_copy(a, g.at[me["x"], me["c"], me["y"], me["z"]], own)
        self.own.start()

    def send(self, p, k, src, dst, dev):
        return remote(src, dst, self.ssem.at[p, k], self.rsem.at[p, k], dev, self.sends)

    def first(self):
        for p in range(3):
            d = ORDERS[p][0]
            dst = view(self.g, self.me, {}, COLS[p])
            src = self.a.at[:, pl.ds(*COLS[p])]
            self.got[p] = [self.send(p, k - 1, src, dst, ring(self.me, d, k)) for k in (1, 3, 2)]

    def second(self):
        self.own.wait()
        for p in range(3):
            for cp in self.got[p]:
                cp.wait_recv()
            d0, d1, _ = ORDERS[p]
            blk = view(self.g, self.me, {d0: ALL}, COLS[p])
            self.got[p] = [self.send(p, 2 + k, blk, blk, ring(self.me, d1, k)) for k in (1, 3, 2)]

    def mate(self, p, k, blk):
        self.mates.append(self.send(p, k, blk, blk, {"c": 1 - self.me["c"]}))

    def third(self):
        for p in range(3):
            for cp in self.got[p]:
                cp.wait_recv()
            d0, d1, d2 = ORDERS[p]
            halves = [view(self.g, self.me, {d0: pl.ds(2 * h, 2), d1: ALL}, COLS[p]) for h in range(2)]
            self.got[p] = {}
            for o in range(2):
                for k, h in ((1, o), (3, 1 - o)):
                    self.got[p][k, h] = self.send(p, 6 + 2 * (k // 2) + h, halves[h], halves[h], ring(self.me, d2, k))
            blk = view(self.g, self.me, {d0: ALL, d1: ALL}, COLS[p])
            self.mate(p, 10, blk)

    def forward(self):
        self.over = [None] * 3
        for p in range(3):
            d0, d1, d2 = ORDERS[p]
            self.over[p] = []
            for k, h in ((1, 0), (3, 1)):
                self.got[p][k, h].wait_recv()
                at = ring(self.me, d2, 4 - k)
                half = view(self.g, self.me, {d0: pl.ds(2 * h, 2), d1: ALL}, COLS[p], at)
                self.over[p].append(self.send(p, 11 + h, half, half, ring(self.me, d2, k)))
        for p in range(3):
            d0, d1, d2 = ORDERS[p]
            for k, h in ((1, 0), (3, 1)):
                self.got[p][k, 1 - h].wait_recv()
                at = ring(self.me, d2, 4 - k)
                self.mate(p, 13 + h, view(self.g, self.me, {d0: ALL, d1: ALL}, COLS[p], at))

    def last(self):
        for p in range(3):
            d0, d1, d2 = ORDERS[p]
            for h in range(2):
                self.over[p][h].wait_recv()
            at = ring(self.me, d2, 2)
            self.mate(p, 15, view(self.g, self.me, {d0: ALL, d1: ALL}, COLS[p], at))

    def finish(self):
        for cp in self.mates:
            cp.wait_recv()
        for cp in self.sends:
            cp.wait_send()


def gather_kernel(t_ref, a_ref, m_ref, tg_ref, ag_ref, mg_ref, ts, tr, as_, ar, ms, mr, own):
    me = greet()
    tok = Gather(t_ref, tg_ref, me, ts, tr, own.at[0])
    tok.first()
    mine = pltpu.make_async_copy(m_ref, mg_ref.at[me["y"], me["z"]], own.at[2])
    mine.start()
    sends = []
    here = mg_ref.at[me["y"], me["z"]]
    got = [remote(m_ref, here, ms.at[k], mr.at[k], ring(me, "z", k + 1), sends) for k in range(3)]
    lead = Gather(a_ref, ag_ref, me, as_, ar, own.at[1])
    lead.first()
    tok.second()
    mine.wait()
    for cp in got:
        cp.wait_recv()
    row = mg_ref.at[me["y"]]
    got = [remote(row, row, ms.at[3 + k], mr.at[3 + k], ring(me, "y", k + 1), sends) for k in range(3)]
    tok.third()
    lead.second()
    tok.forward()
    lead.third()
    tok.last()
    lead.forward()
    tok.finish()
    for cp in got:
        cp.wait_recv()
    lead.last()
    lead.finish()
    for cp in sends:
        cp.wait_send()


def gather_all(tok, lead, meta):
    full = jax.ShapeDtypeStruct((4, 2, 4, 4) + tok.shape, tok.dtype)
    dma = pltpu.SemaphoreType.DMA
    hbm = pl.BlockSpec(memory_space=pl.ANY)
    return pl.pallas_call(
        gather_kernel,
        out_shape=(full, full, jax.ShapeDtypeStruct((4, 4, 8, 128), jnp.float32)),
        in_specs=[hbm] * 3,
        out_specs=[hbm] * 3,
        scratch_shapes=[dma((3, 16))] * 4 + [dma((6,))] * 2 + [dma((3,))],
        compiler_params=pltpu.CompilerParams(collective_id=0, has_side_effects=True),
    )(tok, lead, meta)


def join_kernel(m_ref, s_ref, o_ref, mb, sb, ssem, rsem):
    me = greet()
    mb[0, 0] = m_ref[...]
    sb[0, 0] = s_ref[...]
    sends = []
    stages = [("c", [{"c": 1 - me["c"]}])]
    stages += [(a, [ring(me, a, k) for k in range(1, 4)]) for a in ("x", "y", "z")]
    for i, (a, devs) in enumerate(stages):
        got = []
        for k, dev in enumerate(devs):
            got.append(remote(mb.at[i, 0], mb.at[i, k + 1], ssem.at[0, i, k], rsem.at[0, i, k], dev, sends))
            got.append(remote(sb.at[i, 0], sb.at[i, k + 1], ssem.at[1, i, k], rsem.at[1, i, k], dev, sends))
        for cp in got:
            cp.wait_recv()
        n = len(devs) + 1
        top = mb[i, 0]
        for k in range(1, n):
            top = jnp.maximum(top, mb[i, k])
        total = sb[i, 0] * jnp.exp(mb[i, 0] - top)
        for k in range(1, n):
            total += sb[i, k] * jnp.exp(mb[i, k] - top)
        if i < 3:
            mb[i + 1, 0] = top
            sb[i + 1, 0] = total
    o_ref[0] = top
    o_ref[1] = jnp.log(total)
    for cp in sends:
        cp.wait_send()


def joined(local_max, local_total):
    vm = pl.BlockSpec(memory_space=pltpu.VMEM)
    dma = pltpu.SemaphoreType.DMA
    out = pl.pallas_call(
        join_kernel,
        out_shape=jax.ShapeDtypeStruct((2, 8, 128), jnp.float32),
        in_specs=[vm] * 2,
        out_specs=vm,
        scratch_shapes=[pltpu.VMEM((4, 4, 8, 128), jnp.float32)] * 2 + [dma((2, 4, 3))] * 2,
        compiler_params=pltpu.CompilerParams(collective_id=1, has_side_effects=True),
    )(local_max.reshape(8, 128), local_total.reshape(8, 128))
    return out[0].reshape(-1), out[1].reshape(-1)


def routing(tok, choice, proj):
    ids = choice.T
    scores = lax.dot_general(proj, tok, (((0,), (1,)), ((), ())), preferred_element_type=jnp.float32)
    hot = (ids[:, None, :] == jnp.arange(EX, dtype=jnp.int32)[None, :, None]).astype(jnp.float32)
    picked = jnp.sum(hot * scores[None], axis=1)
    gates = jax.nn.softmax(picked, axis=0)
    n = tok.shape[0]
    before = (jnp.arange(n)[:, None] < jnp.arange(n)[None, :]).astype(jnp.float32)
    earlier = jnp.dot(jnp.sum(hot, axis=0), before, preferred_element_type=jnp.float32)
    slots = jnp.sum(hot * earlier[None], axis=1)
    keys = ids.astype(jnp.float32) * SLOTS + slots
    return jnp.pad(jnp.concatenate([keys, gates], axis=0), ((0, 0), (0, 128 - n)))


def per_device(lead, heat, embed, tok, choice, proj, w_gate, w_up, w_down):
    v = lax.axis_index(VOCAB)
    e = lax.axis_index(EXPERT)
    temp = 0.5 + 0.25 * heat.astype(jnp.float32)
    meta = routing(tok, choice, proj)
    tg, ag, mg = gather_all(lax.dynamic_slice_in_dim(tok, v * 8, 8, 0), lead, meta)
    tokens = tg.reshape(8, 16, 8, -1).transpose(1, 0, 2, 3).reshape(4, 256, -1)
    rows = ag.reshape(1024, -1)
    meta_all = mg.reshape(16, 8, 128)[:, :, :64]
    keys = meta_all[:, :4] - (e * (HOLD * SLOTS)).astype(jnp.float32)
    near = (keys >= 0) & (keys < HOLD * SLOTS)
    keys = jnp.where(near, keys + 32.0 * (jnp.arange(16) % 4)[:, None, None], -1.0)
    keys = keys.reshape(4, 4, 4, 64).transpose(0, 2, 1, 3).reshape(4, 4, 256)
    gates = meta_all[:, 4:].reshape(4, 4, 4, 64).transpose(0, 2, 1, 3).reshape(4, 4, 256)
    eq = keys[:, :, None, :] == jnp.arange(128, dtype=jnp.float32)[None, None, :, None]
    hot = jnp.sum(eq.astype(jnp.float32), axis=1)
    gate_of = jnp.sum(jnp.sum(jnp.where(eq, gates[:, :, None, :], 0.0), axis=1), axis=2)
    hot = hot.astype(jnp.bfloat16)
    picked = jnp.einsum("gst,gtd->gsd", hot, tokens, preferred_element_type=jnp.float32).astype(jnp.bfloat16)
    picked = picked.reshape(16, HOLD, SLOTS, -1)
    gp = jnp.einsum("secd,edf->secf", picked, w_gate, preferred_element_type=jnp.float32)
    up = jnp.einsum("secd,edf->secf", picked, w_up, preferred_element_type=jnp.float32)
    act = (gp * jax.nn.sigmoid(1.702 * gp) * (up + 1.0)).astype(jnp.bfloat16)
    part = jnp.einsum("secf,efd->secd", act, w_down, preferred_element_type=jnp.float32)
    part = part.reshape(4, 128, -1) * gate_of[:, :, None]
    high = part.astype(jnp.bfloat16)
    low = (part - high.astype(jnp.float32)).astype(jnp.bfloat16)
    mixed = jnp.einsum("gst,gsd->gtd", hot, high, preferred_element_type=jnp.float32)
    mixed += jnp.einsum("gst,gsd->gtd", hot, low, preferred_element_type=jnp.float32)
    mixed = mixed.reshape(1024, -1)
    mine = lax.all_to_all(mixed.astype(jnp.bfloat16).reshape(1024, 8, 360).transpose(1, 0, 2), VOCAB, 0, 0, tiled=True)
    mine = jnp.sum(mine.astype(jnp.float32), axis=0).astype(jnp.bfloat16).reshape(16, 64, 360)
    mine = lax.all_to_all(mine, EXPERT, 0, 0, tiled=True)
    moe = jnp.sum(mine.astype(jnp.float32), axis=0).astype(jnp.bfloat16)

    scaled = lax.dot_general(rows, embed, (((1,), (1,)), ((), ())), preferred_element_type=jnp.float32)
    scaled = scaled / temp[:, None]
    top = jnp.max(scaled, axis=1)
    total = jnp.sum(jnp.exp(scaled - top[:, None]), axis=1)
    top, log_total = joined(top, total)
    return scaled - top[:, None] - log_total[:, None], moe


def solution(mesh):
    torus = Mesh(mesh.devices.reshape(4, 2, 4, 4), AXES)
    placed = (
        P(AXES, None), P(), P(AXES, None), P(EXPERT, None), P(EXPERT, None), P(),
        P(EXPERT, None, VOCAB), P(EXPERT, None, VOCAB), P(EXPERT, VOCAB, None),
    )
    return jax.shard_map(
        per_device, mesh=torus, in_specs=placed,
        out_specs=(P(None, AXES), P(EXPERT, VOCAB)), check_vma=False,
    )
```

time: 254 us -> 221 us (0.87)
  Pallas kernels: 0 us -> 99.4 us
  blocking collectives: 85.9 us -> 0 us
  waiting for transfers between devices: 79.3 us -> 5.21 us
  local copies, waits for them, and re-layouts: 28.4 us -> 48.5 us
  matrix products: 26.2 us -> 39.8 us
  between operations: 14.3 us -> 0.86 us
  other arithmetic: 10.5 us -> 16.9 us
    pallas_call x0 -> x2, Pallas kernels: none -> 99.4 us  [the longest x1 57.7 us: joined(): pl.pallas_call(join_kernel, out_shape=jax.ShapeDtypeStruct((2, 8, 128), j...]
    all_to_all x2, waiting for transfers between devices: 78.6 us -> 5.21 us  [the longest x1 5.21 us: per_device(): mine = lax.all_to_all(mine, EXPERT, 0, 0, tiled=True)]
    all_to_all x1 -> x0, blocking collectives: 48.3 us -> none  [per_device(): lax.all_to_all(outgoing, EXPERT, split_axis=0, concat_axis=0, tiled=True)]
    all_gather x4 -> x0, blocking collectives: 37.6 us -> none  [gathered_once(): both, at, found = (lax.all_gather(jnp.concatenate(lines), axis), 0, {})]
    convert_element_type x2 -> x3, local copies, waits for them, and re-layouts: 0.9 us -> 37.8 us  [the longest x2 34.9 us: per_device(): mixed.astype(jnp.bfloat16).reshape(1024, 8, 360).transpose(1, 0, 2)]
    dot_general x5 -> x9, matrix products: 26.2 us -> 39.8 us  [the longest x1 14.7 us: per_device(): lax.dot_general(rows, embed, (((1,), (1,)), ((), ())), preferred_element_...]
    reshape x3 -> x1, local copies, waits for them, and re-layouts: 16.6 us -> 3.57 us  [per_device(): tokens = tg.reshape(8, 16, 8, -1).transpose(1, 0, 2, 3).reshape(4, 256, -1)]
    scatter x1 -> x0, local copies, waits for them, and re-layouts: 4.55 us -> none  [per_device(): outgoing = jnp.zeros((expert_count * capacity, width_full), jnp.bfloat16)...]
  transfers between devices with their start and end apart: 3 -> 2, of which waited for: 2 -> 1; matrix products, arithmetic and copies ran while one was open for 18% -> 11% of each run, Pallas kernels for 0% -> 26%
where the time goes in v1:
time: 221 us; the launch traced here: 220 us
  Pallas kernels  99.4 us (45%)
  local copies, waits for them, and re-layouts  48.5 us (22%)
  matrix products  39.8 us (18%)
  other arithmetic  16.9 us (8%)
  starting transfers between devices  9.08 us (4%)
  waiting for transfers between devices  5.21 us (2%)
    pallas_call x1, Pallas kernels, joined(): pl.pallas_call(join_kernel, out_shape=jax.ShapeDtypeStruct((2, 8, 128), j...  57.7 us
    pallas_call x1, Pallas kernels, gather_all(): pl.pallas_call(gather_kernel, out_shape=(full, full, jax.ShapeDtypeStruct...  41.7 us
    convert_element_type x2, local copies, waits for them, and re-layouts, per_device(): mixed.astype(jnp.bfloat16).reshape(1024, 8, 360).transpose(1, 0, 2)  34.9 us
    dot_general x1, matrix products, per_device(): lax.dot_general(rows, embed, (((1,), (1,)), ((), ())), preferred_element_...  14.7 us
    sub x1, other arithmetic, per_device(): return (scaled - top[:, None] - log_total[:, None], moe)  7.15 us
    dot_general x1, matrix products, per_device(): jnp.einsum('gst,gsd->gtd', hot, high, preferred_element_type=jnp.float32)  6.22 us
    dot_general x1, matrix products, per_device(): jnp.einsum('gst,gsd->gtd', hot, low, preferred_element_type=jnp.float32)  5.55 us
    all_to_all x1, waiting for transfers between devices, per_device(): mine = lax.all_to_all(mine, EXPERT, 0, 0, tiled=True)  5.21 us
  transfers between devices with their start and end apart: 2, of which 1 were waited for; matrix products, arithmetic and copies ran while one was open for 11% of the time, Pallas kernels for 26%

profile of v1, /device:TPU:0, one launch (start us, length us, event | category | flops | bytes accessed | tf_op | source)
XLA Modules:
  0.0 219.7 jit_solution(12932685195362933493)
XLA Ops:
  0.6 0.0 copy-start
  0.7 0.8 convert_reduce_fusion.1
  1.4 0.1 fusion.35
  1.5 0.1 copy-done
  1.6 1.2 fusion.45
  2.9 0.7 select_reduce_fusion.2
  3.7 0.6 constant_dynamic-slice_fusion.t_ref
  4.3 0.7 multiply_add_fusion.1
  5.0 0.6 select_maximum_fusion.m_ref
  5.6 41.7 %shard_map.104 = (bf16[4,2,4,4,8,2880]{5,4,3,2,1,0:T(8,128)(2,1)}, bf16[4,2,4,4,8,2880]{5,4,3,2,1,0:T(8,128)(2,1)}, f32[4,4,8,128]{3,2,1,0:T(8,128)}) custom-call(bf16[8,2880]{1,0:T(8,128)(2,1)} %constant_dynamic-slice_fusion.t_ref, bf16[8,2880]{1,0:T(8,128)(2,1)} %a_ref.1, f32[8,128]{1,0:T(8,128)} %select_maximum_fusion.m_ref), custom_call_target="tpu_custom_call" | custom-call | tf_op jit(solution)/shard_map/pallas_call | solution.py:162
  47.3 0.9 fusion.43
  48.2 0.1 add_select_fusion
  48.3 0.1 reshape.80
  48.4 0.1 reshape.81
  48.5 3.6 %copy.74 = bf16[8,16,8,2880]{3,2,0,1:T(8,128)(2,1)S(1)} copy(bf16[8,16,8,2880]{3,2,1,0:T(8,128)(2,1)} %bitcast.57) | data formatting | bytes 11796480 | tf_op jit(solution)/shard_map/reshape | solution.py:236
  52.1 0.4 select_reduce_fusion
  52.5 2.4 %convolution_convert_fusion = bf16[4,128,2880]{1,2,0:T(8,128)(2,1)S(1)} fusion(bf16[4,256,2880]{2,1,0:T(8,128)(2,1)S(1)} %bitcast.55, bf16[4,128,256]{2,1,0:T(8,128)(2,1)S(1)} %get-tuple-element.9), kind=kOutput, calls=%fused_computation.6 | convolution fusion | flops 756449280 | bytes 9109504 | tf_op jit(solution)/shard_map/gst,gtd->gsd/dot_general | solution.py:248
  54.9 2.9 %copy.76 = bf16[4,128,2880]{2,1,0:T(8,128)(2,1)} copy(bf16[4,128,2880]{1,2,0:T(8,128)(2,1)S(1)} %convolution_convert_fusion) | data formatting | bytes 5898240 | tf_op jit(solution)/shard_map/convert_element_type | solution.py:248
  57.8 4.8 %fusion.10 = f32[16,4,8,180]{3,2,0,1:T(8,128)S(1)} fusion(bf16[4,2880,180,1]{1,0,2,3:T(4,128)(2,1)} %bitcast.71, bf16[16,4,8,2880]{3,2,1,0:T(8,128)(2,1)} %bitcast.61), kind=kOutput, calls=%fused_computation.21 | convolution fusion | flops 530841600 | bytes 7464960 | tf_op jit(solution)/shard_map/secd,edf->secf/dot_general | solution.py:250
  62.6 0.0 copy-done.3
  62.7 0.0 slice-start.1
  62.7 3.8 %fusion.30 = bf16[16,4,8,180]{3,2,0,1:T(8,128)(2,1)S(1)} fusion(bf16[4,2880,180,1]{1,0,2,3:T(4,128)(2,1)} %bitcast.72, bf16[16,4,8,2880]{3,2,1,0:T(8,128)(2,1)S(1)} %bitcast.62, f32[16,4,8,180]{3,2,0,1:T(8,128)S(1)} %fusion.10), kind=kOutput, calls=%fused_computation.25 | convolution fusion | flops 531578880 | bytes 7649280 | tf_op jit(solution)/shard_map/secd,edf->secf/dot_general | solution.py:251
  66.5 0.0 slice-done
  66.5 0.0 slice-done.1
  66.5 1.1 convolution_bitcast_fusion
  67.5 0.7 copy.82
  68.2 6.2 %fusion.5 = f32[4,256,2880]{1,2,0:T(8,128)} fusion(f32[4,128,2880]{2,1,0:T(8,128)S(1)} %bitcast.53, f32[4,128]{1,0:T(4,128)S(1)} %get-tuple-element.8, bf16[4,128,256]{2,1,0:T(8,128)(2,1)S(1)} %get-tuple-element.9), kind=kOutput, calls=%fused_computation.13 | convolution fusion | flops 757923840 | bytes 17958912 | tf_op jit(solution)/shard_map/gst,gsd->gtd/dot_general | solution.py:257
  74.5 5.5 %add_convert_fusion = bf16[4,256,2880]{1,2,0:T(8,128)(2,1)S(1)} fusion(f32[4,256,2880]{1,2,0:T(8,128)} %fusion.5, f32[4,128,2880]{2,1,0:T(8,128)S(1)} %bitcast.54, f32[4,128]{1,0:T(4,128)S(1)} %get-tuple-element.8, bf16[4,128,256]{2,1,0:T(8,128)(2,1)S(1)} %get-tuple-element.9), kind=kOutput, calls=%fused_computation | convolution fusion | flops 768245760 | bytes 23857152 | tf_op jit(solution)/shard_map/gst,gsd->gtd/dot_general | solution.py:258
  80.0 23.7 %copy.87 = bf16[4,256,2880]{1,0,2:T(4,128)(2,1)} copy(bf16[4,256,2880]{1,2,0:T(8,128)(2,1)S(1)} %add_convert_fusion) | data formatting | bytes 11796480 | tf_op jit(solution)/shard_map/convert_element_type | solution.py:260
  103.7 11.2 %convert_element_type.68 = bf16[1024,8,360]{0,2,1:T(8,128)(2,1)} reshape(bf16[4,256,2880]{1,0,2:T(4,128)(2,1)} %copy.87) | data formatting | bytes 11796480 | tf_op jit(solution)/shard_map/convert_element_type | solution.py:260
  114.9 5.1 %all-to-all-start = ((bf16[8,1024,360]{1,2,0:T(8,128)(2,1)}), bf16[8,1024,360]{1,2,0:T(8,128)(2,1)}, u32[]{:S(2)}, u32[]{:S(2)}) async-start(bf16[8,1024,360]{1,2,0:T(8,128)(2,1)} %bitcast.56), calls=%async_computation | async-start | bytes 11796480 | tf_op jit(solution)/shard_map/all_to_all | solution.py:260
  119.9 0.0 copy-done.5
  120.0 14.7 %fusion.44 = (f32[1024]{0:T(1024)S(1)}, f32[1024,1571]{0,1:T(8,128)S(1)}) fusion(f32[1024]{0:T(1024)S(1)} %multiply_add_fusion, bf16[1024,2880]{1,0:T(8,128)(2,1)} %bitcast.70, bf16[1571,2880]{1,0:T(8,128)(2,1)} %param.11), kind=kOutput, calls=%fused_computation.51 | convolution fusion | flops 9269351424 | bytes 21390208 | tf_op jit(solution)/shard_map/dot_general | solution.py:265
  134.7 0.0 copy-start.2
  134.7 0.0 copy-start.4
  134.7 2.7 %copy-done.2 = f32[1024,1571]{0,1:T(8,128)} copy-done((f32[1024,1571]{0,1:T(8,128)}, f32[1024,1571]{0,1:T(8,128)S(1)}, u32[]{:S(2)}) %copy-start.2) | copy-done | bytes 6434840
  137.4 1.6 exponential_reduce_fusion
  139.0 0.0 copy-done.4
  139.0 57.7 %shard_map.105 = f32[2,8,128]{2,1,0:T(8,128)} custom-call(f32[8,128]{1,0:T(8,128)} %bitcast.68, f32[8,128]{1,0:T(8,128)} %bitcast.69), custom_call_target="tpu_custom_call" | custom-call | tf_op jit(solution)/shard_map/pallas_call | solution.py:205
  196.7 0.7 slice_bitcast_fusion.1
  197.3 0.0 all-to-all-done
  197.3 4.1 %reduce_sum.98 = bf16[1024,360]{0,1:T(8,128)(2,1)S(1)} reduce(bf16[8,1024,360]{1,2,0:T(8,128)(2,1)} %all-to-all-done, bf16[]{:T(256)} %constant.68.clone.1), dimensions={0}, to_apply=%region_9.10 | reduce | flops 2580480 | bytes 6635522 | tf_op jit(solution)/shard_map/reduce_sum | solution.py:261
  201.4 1.2 copy.88
  202.6 4.0 %all-to-all-start.1 = ((bf16[16,64,360]{2,1,0:T(8,128)(2,1)}), bf16[16,64,360]{2,1,0:T(8,128)(2,1)S(1)}, u32[]{:S(2)}, u32[]{:S(2)}) async-start(bf16[16,64,360]{2,1,0:T(8,128)(2,1)} %bitcast.23), calls=%async_computation.1 | async-start | bytes 1572864 | tf_op jit(solution)/shard_map/all_to_all | solution.py:262
  206.6 0.0 copy-start.1
  206.6 7.2 %subtract_subtract_fusion = f32[1024,1571]{0,1:T(8,128)} fusion(f32[1024,1571]{0,1:T(8,128)} %copy-done.2, f32[1024]{0:T(1024)S(1)} %get-tuple-element.15, f32[1024]{0:T(1024)S(1)} %get-tuple-element.14), kind=kLoop, calls=%fused_computation.1 | loop fusion | flops 3217408 | bytes 12877824 | tf_op jit(solution)/shard_map/sub | solution.py:270
  213.8 5.2 %all-to-all-done.1 = bf16[16,64,360]{2,1,0:T(8,128)(2,1)S(1)} async-done(((bf16[16,64,360]{2,1,0:T(8,128)(2,1)}), bf16[16,64,360]{2,1,0:T(8,128)(2,1)S(1)}, u32[]{:S(2)}, u32[]{:S(2)}) %all-to-all-start.1) | async-done | bytes 737312 | tf_op jit(solution)/shard_map/all_to_all | solution.py:262
  219.0 0.7 reduce_sum.99
  (12 shorter events, 0.1 us)
Async XLA Ops:
  0.6 1.0 copy-start
  57.8 4.8 %copy-start.3 = (bf16[4,128,2880]{2,1,0:T(8,128)(2,1)S(1)}, bf16[4,128,2880]{2,1,0:T(8,128)(2,1)}, u32[]{:S(2)}) copy-start(bf16[4,128,2880]{2,1,0:T(8,128)(2,1)} %copy.76) | copy-start | bytes 8847364
  57.8 8.6 %slice-start = ((s8[4239360]{0:T(1024)(128)(4,1)}), s8[4194304]{0:T(1024)(128)(4,1)S(1)}, s32[]{:S(2)}) async-start(s8[4239360]{0:T(1024)(128)(4,1)} %bitcast.58), calls=%async_computation.2 | async-start | bytes 8388608
  62.7 3.8 %slice-start.1 = ((s8[4239360]{0:T(1024)(128)(4,1)}), s8[45056]{0:T(1024)(128)(4,1)S(1)}, s32[]{:S(2)}) async-start(s8[4239360]{0:T(1024)(128)(4,1)} %bitcast.58), calls=%async_computation.3 | async-start | bytes 90112
  114.9 5.1 %copy-start.5 = (s32[1024]{0:T(1024)S(1)}, s32[1024]{0:T(1024)}, u32[]{:S(2)}) copy-start(s32[1024]{0:T(1024)} %param.10) | copy-start | bytes 12292
  114.9 82.5 %all-to-all-start = ((bf16[8,1024,360]{1,2,0:T(8,128)(2,1)}), bf16[8,1024,360]{1,2,0:T(8,128)(2,1)}, u32[]{:S(2)}, u32[]{:S(2)}) async-start(bf16[8,1024,360]{1,2,0:T(8,128)(2,1)} %bitcast.56), calls=%async_computation | async-start | bytes 11796480 | tf_op jit(solution)/shard_map/all_to_all | solution.py:260
  134.7 2.8 %copy-start.2 = (f32[1024,1571]{0,1:T(8,128)}, f32[1024,1571]{0,1:T(8,128)S(1)}, u32[]{:S(2)}) copy-start(f32[1024,1571]{0,1:T(8,128)S(1)} %get-tuple-element.17) | copy-start | bytes 19304452
  134.7 4.3 %copy-start.4 = (f32[1024]{0:T(1024)}, f32[1024]{0:T(1024)S(1)}, u32[]{:S(2)}) copy-start(f32[1024]{0:T(1024)S(1)} %get-tuple-element.16) | copy-start | bytes 12292
  202.6 16.4 %all-to-all-start.1 = ((bf16[16,64,360]{2,1,0:T(8,128)(2,1)}), bf16[16,64,360]{2,1,0:T(8,128)(2,1)S(1)}, u32[]{:S(2)}, u32[]{:S(2)}) async-start(bf16[16,64,360]{2,1,0:T(8,128)(2,1)} %bitcast.23), calls=%async_computation.1 | async-start | bytes 1572864 | tf_op jit(solution)/shard_map/all_to_all | solution.py:262
  206.6 13.1 %copy-start.1 = (bf16[64,2880]{1,0:T(8,128)(2,1)S(1)}, bf16[64,2880]{1,0:T(8,128)(2,1)}, u32[]{:S(2)}) copy-start(bf16[64,2880]{1,0:T(8,128)(2,1)} %param.12) | copy-start | bytes 1105924

commit v2 on v1

v2 whole, which is shorter than its diff:
```python
import functools

import jax
import jax.numpy as jnp
from jax import lax
from jax.experimental import pallas as pl
from jax.experimental.pallas import tpu as pltpu
from jax.sharding import Mesh
from jax.sharding import PartitionSpec as P

AXES = ("x", "c", "y", "z")
EXPERT = ("y", "z")
VOCAB = ("x", "c")
MESH = pl.DeviceIdType.MESH
COLS = ((0, 1024), (1024, 1024), (2048, 832))
ORDERS = (("z", "y", "x"), ("x", "z", "y"), ("y", "x", "z"))
EX, HOLD, SLOTS = 64, 4, 8


def ring(me, axis, step):
    return {axis: lax.rem(me[axis] + step, 4)}


def greet():
    me = {a: lax.axis_index(a) for a in AXES}
    barrier = pltpu.get_barrier_semaphore()
    for a in ("x", "y", "z"):
        for k in range(1, 4):
            pl.semaphore_signal(barrier, inc=1, device_id=ring(me, a, k), device_id_type=MESH)
    pl.semaphore_signal(barrier, inc=1, device_id={"c": 1 - me["c"]}, device_id_type=MESH)
    pl.semaphore_wait(barrier, 10)
    return me


def view(g, dims, me, ranges, cols, at={}):
    idx = [ranges.get(a, at.get(a, me[a])) for a in dims]
    return g.at[idx[0], idx[1], idx[2], idx[3], :, pl.ds(*cols)]


def remote(src, dst, ssem, rsem, dev, sends):
    cp = pltpu.make_async_remote_copy(
        src_ref=src, dst_ref=dst, send_sem=ssem, recv_sem=rsem, device_id=dev, device_id_type=MESH
    )
    cp.start()
    sends.append(cp)
    return cp


ALL = pl.ds(0, 4)


class Gather:
    def __init__(self, a, g, dims, me, ssem, rsem, own):
        self.dims = dims
        self.a, self.g, self.me, self.ssem, self.rsem = a, g, me, ssem, rsem
        self.sends, self.mates, self.got = [], [], [None] * 3
        self.own = pltpu.make_async_copy(a, g.at[tuple(me[d] for d in dims)], own)
        self.own.start()

    def send(self, p, k, src, dst, dev):
        return remote(src, dst, self.ssem.at[p, k], self.rsem.at[p, k], dev, self.sends)

    def first(self):
        for p in range(3):
            d = ORDERS[p][0]
            dst = view(self.g, self.dims, self.me, {}, COLS[p])
            src = self.a.at[:, pl.ds(*COLS[p])]
            self.got[p] = [self.send(p, k - 1, src, dst, ring(self.me, d, k)) for k in (1, 3, 2)]

    def second(self):
        self.own.wait()
        for p in range(3):
            for cp in self.got[p]:
                cp.wait_recv()
            d0, d1, _ = ORDERS[p]
            blk = view(self.g, self.dims, self.me, {d0: ALL}, COLS[p])
            self.got[p] = [self.send(p, 2 + k, blk, blk, ring(self.me, d1, k)) for k in (1, 3, 2)]

    def mate(self, p, k, blk):
        self.mates.append(self.send(p, k, blk, blk, {"c": 1 - self.me["c"]}))

    def third(self):
        for p in range(3):
            for cp in self.got[p]:
                cp.wait_recv()
            d0, d1, d2 = ORDERS[p]
            halves = [view(self.g, self.dims, self.me, {d0: pl.ds(2 * h, 2), d1: ALL}, COLS[p]) for h in range(2)]
            self.got[p] = {}
            for o in range(2):
                for k, h in ((1, o), (3, 1 - o)):
                    self.got[p][k, h] = self.send(p, 6 + 2 * (k // 2) + h, halves[h], halves[h], ring(self.me, d2, k))
            blk = view(self.g, self.dims, self.me, {d0: ALL, d1: ALL}, COLS[p])
            self.mate(p, 10, blk)

    def forward(self):
        self.over = [None] * 3
        for p in range(3):
            d0, d1, d2 = ORDERS[p]
            self.over[p] = []
            for k, h in ((1, 0), (3, 1)):
                self.got[p][k, h].wait_recv()
                at = ring(self.me, d2, 4 - k)
                half = view(self.g, self.dims, self.me, {d0: pl.ds(2 * h, 2), d1: ALL}, COLS[p], at)
                self.over[p].append(self.send(p, 11 + h, half, half, ring(self.me, d2, k)))
        for p in range(3):
            d0, d1, d2 = ORDERS[p]
            for k, h in ((1, 0), (3, 1)):
                self.got[p][k, 1 - h].wait_recv()
                at = ring(self.me, d2, 4 - k)
                self.mate(p, 13 + h, view(self.g, self.dims, self.me, {d0: ALL, d1: ALL}, COLS[p], at))

    def last(self):
        for p in range(3):
            d0, d1, d2 = ORDERS[p]
            for h in range(2):
                self.over[p][h].wait_recv()
            at = ring(self.me, d2, 2)
            self.mate(p, 15, view(self.g, self.dims, self.me, {d0: ALL, d1: ALL}, COLS[p], at))

    def arrive(self):
        for cp in self.mates:
            cp.wait_recv()

    def drain(self):
        for cp in self.sends:
            cp.wait_send()


def plan(meta_row, base):
    slot = lax.broadcasted_iota(jnp.int32, (128, 256), 0).astype(jnp.float32)
    src = (lax.broadcasted_iota(jnp.int32, (1, 256), 1) // 64).astype(jnp.float32) * 32.0
    hot = jnp.zeros((128, 256), jnp.float32)
    gates = jnp.zeros((128, 256), jnp.float32)
    for k in range(4):
        key = meta_row[k : k + 1] - base
        key = jnp.where((key >= 0.0) & (key < 32.0), key + src, -1.0)
        eq = slot == key
        hot += jnp.where(eq, 1.0, 0.0)
        gates += jnp.where(eq, meta_row[4 + k : 5 + k], 0.0)
    return hot.astype(jnp.bfloat16), jnp.sum(gates, axis=1, keepdims=True)


def copy(src, dst, sem):
    cp = pltpu.make_async_copy(src, dst, sem)
    cp.start()
    return cp


def dot(a, b, ca, cb):
    return lax.dot_general(a, b, (((ca,), (cb,)), ((), ())), preferred_element_type=jnp.float32)


def a_kernel(
    t_ref, a_ref, m_ref, wg_ref, wu_ref, wd_ref,
    ag_ref, tg_ref, act_ref, mg_ref, wdp_ref,
    wg, wu, wraw, wdp, mg, tok, xs,
    ts, tr, as_, ar, ms, mr, own, rawsem, outsem, toksem,
):
    me = greet()
    tok_g = Gather(t_ref, tg_ref, ("y", "z", "x", "c"), me, ts, tr, own.at[0])
    tok_g.first()
    mine = copy(m_ref, mg.at[me["y"], me["z"]], own.at[2])
    raw = copy(wd_ref, wraw, rawsem.at[0])
    sends = []
    here = mg.at[me["y"], me["z"]]
    mgot = [remote(m_ref, here, ms.at[k], mr.at[k], ring(me, "z", k + 1), sends) for k in range(3)]
    lead = Gather(a_ref, ag_ref, AXES, me, as_, ar, own.at[1])
    lead.first()
    raw.wait()
    tok_g.second()

    def low(i, _):
        r = wraw[pl.ds(i * 4, 4)].reshape(16, 2880)
        for v in range(8):
            rows = pl.ds(pl.multiple_of(i * 16, 16), 16)
            wdp[v % 2, rows, pl.ds((v // 2) * 384, 360)] = r[:, 360 * v : 360 * v + 360]
            wdp[v % 2, rows, pl.ds((v // 2) * 384 + 360, 24)] = jnp.zeros((16, 24), jnp.bfloat16)
        return 0

    lax.fori_loop(0, 45, low, 0)
    low_out = copy(wdp, wdp_ref, outsem.at[0])
    mine.wait()
    for cp in mgot:
        cp.wait_recv()
    row = mg.at[me["y"]]
    mgot = [remote(row, row, ms.at[3 + k], mr.at[3 + k], ring(me, "y", k + 1), sends) for k in range(3)]
    raw = copy(wg_ref, wraw, rawsem.at[1])
    tok_g.third()
    lead.second()
    raw.wait()

    def flat(dst):
        def body(i, _):
            dst[pl.ds(pl.multiple_of(i * 16, 16), 16), :] = wraw[pl.ds(i * 4, 4)].reshape(16, 2880)
            return 0

        lax.fori_loop(0, 45, body, 0)

    flat(wg)
    raw = copy(wu_ref, wraw, rawsem.at[2])
    tok_g.forward()
    lead.third()
    raw.wait()
    flat(wu)
    tok_g.last()
    tok_g.arrive()
    for cp in mgot:
        cp.wait_recv()
    mg_out = copy(mg, mg_ref, outsem.at[1])
    base = ((me["y"] * 4 + me["z"]) * 32).astype(jnp.float32)
    flat_tok = tg_ref.reshape(1024, 2880)
    loads = [copy(flat_tok.at[pl.ds(0, 256)], tok.at[0], toksem.at[0])]
    for g in range(4):
        if g < 3:
            loads.append(copy(flat_tok.at[pl.ds(256 * (g + 1), 256)], tok.at[(g + 1) % 2], toksem.at[g + 1]))
        loads[g].wait()
        row = jnp.concatenate([mg[g, 0] + mg[g, 1], mg[g, 2] + mg[g, 3]], axis=1)
        hot, _ = plan(row, base)
        xs[pl.ds(128 * g, 128), :] = dot(hot, tok[g % 2], 1, 0).astype(jnp.bfloat16)
    lead.forward()

    def ffn(i, _):
        rows = pl.ds(pl.multiple_of(i * 128, 128), 128)
        x = xs[rows, :]
        gp = dot(x, wg[...], 1, 1)
        up = dot(x, wu[...], 1, 1)
        r = lax.broadcasted_iota(jnp.int32, (128, 720), 0)
        c = lax.broadcasted_iota(jnp.int32, (128, 720), 1)
        keep = lax.rem(lax.div(r, 8), 4) == lax.rem(c, 4)
        h = gp * jax.nn.sigmoid(1.702 * gp) * (up + 1.0)
        act_ref[rows, :] = jnp.where(keep, h, 0.0).astype(jnp.bfloat16)
        return 0

    lax.fori_loop(0, 4, ffn, 0)
    lead.last()
    lead.arrive()
    low_out.wait()
    mg_out.wait()
    tok_g.drain()
    lead.drain()
    for cp in sends:
        cp.wait_send()


def kernel_a(tok, lead, meta, w_gate, w_up, w_down):
    bf = jnp.bfloat16
    full = jax.ShapeDtypeStruct((4, 2, 4, 4, 8, 2880), bf)
    tfull = jax.ShapeDtypeStruct((4, 4, 4, 2, 8, 2880), bf)
    dma = pltpu.SemaphoreType.DMA
    hbm = pl.BlockSpec(memory_space=pl.ANY)
    vm = pl.BlockSpec(memory_space=pltpu.VMEM)
    return pl.pallas_call(
        a_kernel,
        out_shape=(
            full, tfull, jax.ShapeDtypeStruct((512, 720), bf),
            jax.ShapeDtypeStruct((4, 4, 8, 128), jnp.float32), jax.ShapeDtypeStruct((2, 720, 1536), bf),
        ),
        in_specs=[hbm] * 6,
        out_specs=[hbm, hbm, vm, hbm, hbm],
        scratch_shapes=[
            pltpu.VMEM((720, 2880), bf), pltpu.VMEM((720, 2880), bf), pltpu.VMEM((180, 4, 2880), bf),
            pltpu.VMEM((2, 720, 1536), bf), pltpu.VMEM((4, 4, 8, 128), jnp.float32),
            pltpu.VMEM((2, 256, 2880), bf), pltpu.VMEM((512, 2880), bf),
        ]
        + [dma((3, 16))] * 4 + [dma((6,))] * 2 + [dma((3,)), dma((3,)), dma((2,)), dma((4,))],
        compiler_params=pltpu.CompilerParams(collective_id=0, has_side_effects=True, vmem_limit_bytes=60 * 2**20),
    )(tok, lead, meta, w_gate, w_up, w_down)


BACK = (("z", "y", "x"), ("x", "z", "y"), ("y", "x", "z"))
DEST = ("x", "y", "z")
VB, NV, VOC = 392, 4, 1571


def b_kernel(
    act_ref, m_ref, it_ref, wdp_ref, emb_ref, ag_ref,
    sc_ref, st_ref, moe_ref,
    wd, emb, rows, lg, to_mate, from_mate, own, out1, in1, sum1, out2, in2, sum2, out3, in3, mb, sb,
    wsem, esem, xsem, lsem, hs, hr, s1, r1, s2, r2, s3, r3, ssem, rsem,
):
    c = lax.axis_index("c")
    wload = [copy(wdp_ref.at[1 - c], wd.at[0], wsem.at[0]), copy(wdp_ref.at[c], wd.at[1], wsem.at[1])]
    eload = copy(emb_ref, emb, esem)
    flat = ag_ref.reshape(1024, 2880)
    xload = [copy(flat.at[pl.ds(256 * i, 256)], rows.at[i], xsem.at[i]) for i in range(2)]
    me = greet()
    sends = []
    base = ((me["y"] * 4 + me["z"]) * 32).astype(jnp.float32)
    mate = {"c": 1 - me["c"]}
    hgot = []
    for half in range(2):
        wload[half].wait()
        for g in range(4):
            row = jnp.concatenate([m_ref[g, 0] + m_ref[g, 1], m_ref[g, 2] + m_ref[g, 3]], axis=1)
            hot, gate = plan(row, base)
            y = dot(act_ref[pl.ds(128 * g, 128), :], wd[half], 1, 0) * gate
            high = y.astype(jnp.bfloat16)
            low = (y - high.astype(jnp.float32)).astype(jnp.bfloat16)
            mix = dot(jnp.concatenate([hot, hot], axis=0), jnp.concatenate([high, low], axis=0), 0, 0)
            for x in range(4):
                for p in range(3):
                    piece = mix[:, 384 * x + 128 * p : 384 * x + 128 * (p + 1)].reshape(4, 64, 128)
                    if half == 0:
                        to_mate[p, x, g] = piece.astype(jnp.bfloat16)
                    else:
                        own[p, x, g] = piece
            if half == 0:
                hgot.append(remote(to_mate.at[:, :, g], from_mate.at[:, :, g], hs.at[g], hr.at[g], mate, sends))
    for cp in hgot:
        cp.wait_recv()

    def index(p, at, full):
        return (p,) + tuple(at[d] if d in at else pl.ds(0, 4) for d in full)

    got1 = []
    for p in range(3):
        d = BACK[p][0]
        rest = [a for a in DEST if a != d]
        for k in (1, 3, 2):
            i = index(p, ring(me, d, k), DEST)
            out1[p, k - 1] = (own[i] + from_mate[i].astype(jnp.float32)).astype(jnp.bfloat16)
            got1.append((p, k, remote(out1.at[p, k - 1], in1.at[p, k - 1], s1.at[p, k - 1], r1.at[p, k - 1], ring(me, d, k), sends)))
        i = index(p, {d: me[d]}, DEST)
        sum1[p] = own[i] + from_mate[i].astype(jnp.float32)

    eload.wait()
    stores = []
    for j in range(4):
        xload[j].wait()
        inv = it_ref[:, pl.ds(256 * j, 256)]
        if j >= 2:
            stores[j - 2].wait()
        buf = lg.at[j % 2]

        def block(i0, n, top):
            r = dot(emb[pl.ds(i0, n), :], rows[j % 2], 1, 1) * inv
            buf[pl.ds(i0, n), :] = r
            return jnp.maximum(top, jnp.max(r, axis=0, keepdims=True))

        top = jnp.full((1, 256), -jnp.inf, jnp.float32)
        top = lax.fori_loop(0, NV, lambda i, t: block(pl.multiple_of(i * VB, 8), VB, t), top)
        top = block(NV * VB, VOC - NV * VB, top)
        if j < 2:
            xload.append(copy(flat.at[pl.ds(256 * (j + 2), 256)], rows.at[j], xsem.at[j + 2]))

        def tail(i, s):
            return s + jnp.sum(jnp.exp(buf[pl.ds(pl.multiple_of(i * 112, 8), 112), :] - top), axis=0, keepdims=True)

        total = lax.fori_loop(0, 14, tail, jnp.zeros((1, 256), jnp.float32))
        total += jnp.sum(jnp.exp(buf[pl.ds(1568, 3), :] - top), axis=0, keepdims=True)
        for h in range(2):
            mb[0, 0, pl.ds(2 * j + h, 1), :] = top[:, 128 * h : 128 * (h + 1)]
            sb[0, 0, pl.ds(2 * j + h, 1), :] = total[:, 128 * h : 128 * (h + 1)]
        stores.append(copy(buf, sc_ref.at[:, pl.ds(256 * j, 256)], lsem.at[j]))

    stages = [[mate]] + [[ring(me, a, k) for k in range(1, 4)] for a in DEST]

    def begin(i):
        got = []
        for k, dev in enumerate(stages[i]):
            got.append(remote(mb.at[i, 0], mb.at[i, k + 1], ssem.at[0, i, k], rsem.at[0, i, k], dev, sends))
            got.append(remote(sb.at[i, 0], sb.at[i, k + 1], ssem.at[1, i, k], rsem.at[1, i, k], dev, sends))
        return got

    def end(i, got):
        for cp in got:
            cp.wait_recv()
        n = len(stages[i]) + 1
        top = mb[i, 0]
        for k in range(1, n):
            top = jnp.maximum(top, mb[i, k])
        total = sb[i, 0] * jnp.exp(mb[i, 0] - top)
        for k in range(1, n):
            total += sb[i, k] * jnp.exp(mb[i, k] - top)
        if i < 3:
            mb[i + 1, 0] = top
            sb[i + 1, 0] = total
        else:
            st_ref[...] = top + jnp.log(total)

    got = begin(0)
    for p, k, cp in got1:
        cp.wait_recv()
        sum1[p] += in1[p, k - 1].astype(jnp.float32)
    got2 = []
    for p in range(3):
        _, d, e = BACK[p]
        first = [a for a in DEST if a != BACK[p][0]]
        for k in (1, 3, 2):
            i = index(p, ring(me, d, k), first)
            out2[p, k - 1] = sum1[i].astype(jnp.bfloat16)
            got2.append((p, k, remote(out2.at[p, k - 1], in2.at[p, k - 1], s2.at[p, k - 1], r2.at[p, k - 1], ring(me, d, k), sends)))
        sum2[p] = sum1[index(p, {d: me[d]}, first)]
    end(0, got)
    got = begin(1)
    for p, k, cp in got2:
        cp.wait_recv()
        sum2[p] += in2[p, k - 1].astype(jnp.float32)
    got3 = []
    for p in range(3):
        d = BACK[p][2]
        for k in (1, 3, 2):
            out3[p, k - 1] = sum2[p, lax.rem(me[d] + k, 4)]
            got3.append((p, k, remote(out3.at[p, k - 1], in3.at[p, k - 1], s3.at[p, k - 1], r3.at[p, k - 1], ring(me, d, k), sends)))
    end(1, got)
    got = begin(2)
    for p, k, cp in got3:
        cp.wait_recv()
    for p in range(3):
        total = sum2[p, me[BACK[p][2]]]
        for k in range(3):
            total += in3[p, k]
        n = 128 if p < 2 else 104
        moe_ref[:, pl.ds(128 * p, n)] = total[:, :n].astype(jnp.bfloat16)
    end(2, got)
    got = begin(3)
    stores[2].wait()
    stores[3].wait()
    end(3, got)
    for cp in sends:
        cp.wait_send()


def kernel_b(act, meta, inv_temp, wdp, embed, lead):
    bf, f32 = jnp.bfloat16, jnp.float32
    dma = pltpu.SemaphoreType.DMA
    hbm = pl.BlockSpec(memory_space=pl.ANY)
    vm = pl.BlockSpec(memory_space=pltpu.VMEM)
    V = pltpu.VMEM
    return pl.pallas_call(
        b_kernel,
        out_shape=(
            jax.ShapeDtypeStruct((VOC, 1024), f32), jax.ShapeDtypeStruct((8, 128), f32),
            jax.ShapeDtypeStruct((64, 360), bf),
        ),
        in_specs=[vm, vm, vm, hbm, hbm, hbm],
        out_specs=[hbm, vm, vm],
        scratch_shapes=[
            V((2, 720, 1536), bf), V((VOC, 2880), bf), V((2, 256, 2880), bf), V((2, VOC, 256), f32),
            V((3, 4, 4, 4, 64, 128), bf), V((3, 4, 4, 4, 64, 128), bf), V((3, 4, 4, 4, 64, 128), f32),
            V((3, 3, 4, 4, 64, 128), bf), V((3, 3, 4, 4, 64, 128), bf), V((3, 4, 4, 64, 128), f32),
            V((3, 3, 4, 64, 128), bf), V((3, 3, 4, 64, 128), bf), V((3, 4, 64, 128), f32),
            V((3, 3, 64, 128), f32), V((3, 3, 64, 128), f32),
            V((4, 4, 8, 128), f32), V((4, 4, 8, 128), f32),
            dma((2,)), dma, dma((4,)), dma((4,)), dma((4,)), dma((4,)),
        ]
        + [dma((3, 3))] * 6 + [dma((2, 4, 3))] * 2,
        compiler_params=pltpu.CompilerParams(collective_id=1, has_side_effects=True, vmem_limit_bytes=63 * 2**20),
    )(act, meta, inv_temp, wdp, embed, lead)


def c_kernel(s_ref, t_ref, o_ref):
    o_ref[...] = s_ref[...] - t_ref[...]


def kernel_c(scaled, shift):
    n = 200
    blk = pl.BlockSpec((n, 1024), lambda i: (i, 0))
    return pl.pallas_call(
        c_kernel, grid=(pl.cdiv(VOC, n),), out_shape=jax.ShapeDtypeStruct((VOC, 1024), jnp.float32),
        in_specs=[blk, pl.BlockSpec((1, 1024), lambda i: (0, 0))], out_specs=blk,
    )(scaled, shift)


def routing(tok, choice, proj):
    ids = choice.T
    scores = lax.dot_general(proj, tok, (((0,), (1,)), ((), ())), preferred_element_type=jnp.float32)
    hot = (ids[:, None, :] == jnp.arange(EX, dtype=jnp.int32)[None, :, None]).astype(jnp.float32)
    picked = jnp.sum(hot * scores[None], axis=1)
    gates = jax.nn.softmax(picked, axis=0)
    n = tok.shape[0]
    before = (jnp.arange(n)[:, None] < jnp.arange(n)[None, :]).astype(jnp.float32)
    earlier = jnp.dot(jnp.sum(hot, axis=0), before, preferred_element_type=jnp.float32)
    slots = jnp.sum(hot * earlier[None], axis=1)
    keys = ids.astype(jnp.float32) * SLOTS + slots
    both = jnp.concatenate([keys, gates], axis=0)
    odd = lax.axis_index("z") % 2 == 1
    zero = jnp.zeros_like(both)
    return jnp.concatenate([jnp.where(odd, zero, both), jnp.where(odd, both, zero)], axis=1)


def per_device(lead, heat, embed, tok, choice, proj, w_gate, w_up, w_down):
    v = lax.axis_index(VOCAB)
    inv_temp = (1.0 / (0.5 + 0.25 * heat.astype(jnp.float32))).reshape(1, 1024)
    meta = routing(tok, choice, proj)
    flip = lambda w: jnp.transpose(w, (2, 0, 1))
    mine = lax.dynamic_slice_in_dim(tok, v * 8, 8, 0)
    rows, _, act, keys, wdp = kernel_a(
        mine, lead, meta, flip(w_gate), flip(w_up), jnp.transpose(w_down, (1, 0, 2))
    )
    scaled, shift, moe = kernel_b(act, keys, inv_temp, wdp, embed, rows)
    return kernel_c(scaled, shift.reshape(1, 1024)).T, moe


def solution(mesh):
    torus = Mesh(mesh.devices.reshape(4, 2, 4, 4), AXES)
    placed = (
        P(AXES, None), P(), P(AXES, None), P(EXPERT, None), P(EXPERT, None), P(),
        P(EXPERT, None, VOCAB), P(EXPERT, None, VOCAB), P(EXPERT, VOCAB, None),
    )
    return jax.shard_map(
        per_device, mesh=torus, in_specs=placed,
        out_specs=(P(None, AXES), P(EXPERT, VOCAB)), check_vma=False,
    )
```

time: 221 us -> 113 us (0.51)
  local copies, waits for them, and re-layouts: 48.5 us -> 1.26 us
  matrix products: 39.8 us -> 1.38 us
  other arithmetic: 16.9 us -> 4.19 us
  starting transfers between devices: 9.08 us -> 0 us
  Pallas kernels: 99.4 us -> 105 us
  waiting for transfers between devices: 5.21 us -> 0 us
    dot_general x7 -> x0, matrix products: 38.5 us -> none  [the longest x1 14.7 us: per_device(): lax.dot_general(rows, embed, (((1,), (1,)), ((), ())), preferred_element_...]
    convert_element_type x3 -> x0, local copies, waits for them, and re-layouts: 37.8 us -> none  [the longest x2 34.9 us: per_device(): mixed.astype(jnp.bfloat16).reshape(1024, 8, 360).transpose(1, 0, 2)]
    all_to_all x2 -> x0, starting transfers between devices: 9.08 us -> none  [the longest x1 5.06 us: per_device(): lax.all_to_all(mixed.astype(jnp.bfloat16).reshape(1024, 8, 360).transpose...]
    sub x1 -> x0, other arithmetic: 7.15 us -> none  [per_device(): return (scaled - top[:, None] - log_total[:, None], moe)]
    reduce_sum x4 -> x0, other arithmetic: 6.82 us -> none  [the longest x1 4.09 us: per_device(): jnp.sum(mine.astype(jnp.float32), axis=0).astype(jnp.bfloat16)]
    pallas_call x2 -> x3, Pallas kernels: 99.4 us -> 105 us  [the longest x1 53.6 us: kernel_a(): pl.pallas_call(a_kernel, out_shape=(full, tfull, jax.ShapeDtypeStruct((51...]
    all_to_all x2 -> x0, waiting for transfers between devices: 5.21 us -> none  [the longest x1 5.21 us: per_device(): mine = lax.all_to_all(mine, EXPERT, 0, 0, tiled=True)]
    reshape x1 -> x0, local copies, waits for them, and re-layouts: 3.57 us -> none  [per_device(): tokens = tg.reshape(8, 16, 8, -1).transpose(1, 0, 2, 3).reshape(4, 256, -1)]
  transfers between devices with their start and end apart: 2 -> 0, of which waited for: 1 -> 0; matrix products, arithmetic and copies ran while one was open for 11% -> 0% of each run, Pallas kernels for 26% -> 0%
where the time goes in v2:
time: 113 us; the launch traced here: 112 us
  Pallas kernels  105 us (93%)
  other arithmetic  4.19 us (4%)
  matrix products  1.38 us (1%)
  local copies, waits for them, and re-layouts  1.26 us (1%)
    pallas_call x1, Pallas kernels, kernel_a(): pl.pallas_call(a_kernel, out_shape=(full, tfull, jax.ShapeDtypeStruct((51...  53.6 us
    pallas_call x1, Pallas kernels, kernel_b(): pl.pallas_call(b_kernel, out_shape=(jax.ShapeDtypeStruct((VOC, 1024), f32...  43.3 us
    pallas_call x1, Pallas kernels, kernel_c(): pl.pallas_call(c_kernel, grid=(pl.cdiv(VOC, n),), out_shape=jax.ShapeDtyp...  7.93 us

profile of v2, /device:TPU:0, one launch (start us, length us, event | category | flops | bytes accessed | tf_op | source)
XLA Modules:
  0.0 112.3 jit_solution(14714734957832263761)
XLA Ops:
  0.6 0.0 copy-start
  0.7 1.3 %add_divide_fusion = f32[1024]{0:T(1024)} fusion(s32[1024]{0:T(1024)} %param.10), kind=kLoop, calls=%fused_computation.8 | loop fusion | flops 4096 | bytes 8192 | tf_op jit(solution)/shard_map/div | solution.py:484
  2.0 0.7 convert_reduce_fusion
  2.7 0.1 fusion
  2.8 0.0 copy-done
  2.8 1.2 %fusion.5 = f32[64,64]{1,0:T(8,128)S(1)} fusion(bf16[2880,64]{0,1:T(8,128)(2,1)} %param.14, bf16[64,2880]{1,0:T(8,128)(2,1)S(1)} %copy-done), kind=kOutput, calls=%fused_computation.16 | convolution fusion | flops 23592960 | bytes 753664 | tf_op jit(solution)/shard_map/dot_general | solution.py:467
  4.1 0.7 select_reduce_fusion.1
  4.9 0.7 multiply_add_fusion
  5.6 0.7 pad_maximum_fusion.1.m_ref
  6.2 0.6 constant_dynamic-slice_fusion.t_ref
  6.9 53.6 %shard_map.104 = (bf16[4,2,4,4,8,2880]{5,4,3,2,1,0:T(8,128)(2,1)}, bf16[4,4,4,2,8,2880]{5,4,3,2,1,0:T(8,128)(2,1)}, bf16[512,720]{1,0:T(8,128)(2,1)}, f32[4,4,8,128]{3,2,1,0:T(8,128)}, bf16[2,720,1536]{2,1,0:T(8,128)(2,1)}) custom-call(bf16[8,2880]{1,0:T(8,128)(2,1)} %constant_dynamic-slice_fusion.t_ref, bf16[8,2880]{1,0:T(8,128)(2,1)} %a_ref.1, ...), custom_call_target="tpu_custom_call" | custom-call | tf_op jit(solution)/shard_map/pallas_call | solution.py:252
  60.4 43.3 %shard_map.105 = (f32[1571,1024]{1,0:T(8,128)}, f32[8,128]{1,0:T(8,128)}, bf16[64,360]{1,0:T(8,128)(2,1)}) custom-call(bf16[512,720]{1,0:T(8,128)(2,1)} %get-tuple-element.9.act_ref, f32[4,4,8,128]{3,2,1,0:T(8,128)} %get-tuple-element.10.m_ref, f32[1,1024]{1,0:T(1,128)} %bitcast.17, bf16[2,720,1536]{2,1,0:T(8,128)(2,1)} %get-tuple-element.11.wdp_ref, ...), custom_call_target="tpu_custom_call" | custom-call | tf_op jit(solution)/shard_map/pallas_call | solution.py:430
  103.8 0.0 copy-start.1
  103.8 7.9 %shard_map.106 = f32[1571,1024]{1,0:T(8,128)} custom-call(f32[1571,1024]{1,0:T(8,128)} %get-tuple-element.13.s_ref, f32[1,1024]{1,0:T(1,128)} %bitcast.18), custom_call_target="tpu_custom_call" | custom-call | tf_op jit(solution)/shard_map/pallas_call | solution.py:459
  111.7 0.0 copy-done.1
  111.7 0.6 copy.12
  (3 shorter events, 0.1 us)
Async XLA Ops:
  0.6 2.2 %copy-start = (bf16[64,2880]{1,0:T(8,128)(2,1)S(1)}, bf16[64,2880]{1,0:T(8,128)(2,1)}, u32[]{:S(2)}) copy-start(bf16[64,2880]{1,0:T(8,128)(2,1)} %param.12) | copy-start | bytes 1105924
  103.8 7.9 %copy-start.1 = (bf16[64,360]{1,0:T(8,128)(2,1)S(1)}, bf16[64,360]{1,0:T(8,128)(2,1)}, u32[]{:S(2)}) copy-start(bf16[64,360]{1,0:T(8,128)(2,1)} %get-tuple-element.25) | copy-start | bytes 138244

commit v3 on v2

v3 whole, which is shorter than its diff:
```python
import functools

import jax
import jax.numpy as jnp
from jax import lax
from jax.experimental import pallas as pl
from jax.experimental.pallas import tpu as pltpu
from jax.sharding import Mesh
from jax.sharding import PartitionSpec as P

AXES = ("x", "c", "y", "z")
EXPERT = ("y", "z")
VOCAB = ("x", "c")
MESH = pl.DeviceIdType.MESH
COLS = ((0, 1024), (1024, 1024), (2048, 832))
ORDERS = (("z", "y", "x"), ("x", "z", "y"), ("y", "x", "z"))
EX, HOLD, SLOTS = 64, 4, 8


def ring(me, axis, step):
    return {axis: lax.rem(me[axis] + step, 4)}


def greet():
    me = {a: lax.axis_index(a) for a in AXES}
    barrier = pltpu.get_barrier_semaphore()
    for a in ("x", "y", "z"):
        for k in range(1, 4):
            pl.semaphore_signal(barrier, inc=1, device_id=ring(me, a, k), device_id_type=MESH)
    pl.semaphore_signal(barrier, inc=1, device_id={"c": 1 - me["c"]}, device_id_type=MESH)
    pl.semaphore_wait(barrier, 10)
    return me


def view(g, dims, me, ranges, cols, at={}):
    idx = [ranges.get(a, at.get(a, me[a])) for a in dims]
    return g.at[idx[0], idx[1], idx[2], idx[3], :, pl.ds(*cols)]


def remote(src, dst, ssem, rsem, dev, sends):
    cp = pltpu.make_async_remote_copy(
        src_ref=src, dst_ref=dst, send_sem=ssem, recv_sem=rsem, device_id=dev, device_id_type=MESH
    )
    cp.start()
    sends.append(cp)
    return cp


ALL = pl.ds(0, 4)


class Gather:
    def __init__(self, a, g, dims, me, ssem, rsem, own):
        self.dims = dims
        self.a, self.g, self.me, self.ssem, self.rsem = a, g, me, ssem, rsem
        self.sends, self.mates, self.got = [], [], [None] * 3
        self.own = pltpu.make_async_copy(a, g.at[tuple(me[d] for d in dims)], own)
        self.own.start()

    def send(self, p, k, src, dst, dev):
        return remote(src, dst, self.ssem.at[p, k], self.rsem.at[p, k], dev, self.sends)

    def first(self):
        for p in range(3):
            d = ORDERS[p][0]
            dst = view(self.g, self.dims, self.me, {}, COLS[p])
            src = self.a.at[:, pl.ds(*COLS[p])]
            self.got[p] = [self.send(p, k - 1, src, dst, ring(self.me, d, k)) for k in (1, 3, 2)]

    def second(self):
        self.own.wait()
        for p in range(3):
            for cp in self.got[p]:
                cp.wait_recv()
            d0, d1, _ = ORDERS[p]
            blk = view(self.g, self.dims, self.me, {d0: ALL}, COLS[p])
            self.got[p] = [self.send(p, 2 + k, blk, blk, ring(self.me, d1, k)) for k in (1, 3, 2)]

    def mate(self, p, k, blk):
        self.mates.append(self.send(p, k, blk, blk, {"c": 1 - self.me["c"]}))

    def third(self):
        for p in range(3):
            for cp in self.got[p]:
                cp.wait_recv()
            d0, d1, d2 = ORDERS[p]
            halves = [view(self.g, self.dims, self.me, {d0: pl.ds(2 * h, 2), d1: ALL}, COLS[p]) for h in range(2)]
            self.got[p] = {}
            for o in range(2):
                for k, h in ((1, o), (3, 1 - o)):
                    self.got[p][k, h] = self.send(p, 6 + 2 * (k // 2) + h, halves[h], halves[h], ring(self.me, d2, k))
            blk = view(self.g, self.dims, self.me, {d0: ALL, d1: ALL}, COLS[p])
            self.mate(p, 10, blk)

    def forward(self):
        self.over = [None] * 3
        for p in range(3):
            d0, d1, d2 = ORDERS[p]
            self.over[p] = []
            for k, h in ((1, 0), (3, 1)):
                self.got[p][k, h].wait_recv()
                at = ring(self.me, d2, 4 - k)
                half = view(self.g, self.dims, self.me, {d0: pl.ds(2 * h, 2), d1: ALL}, COLS[p], at)
                self.over[p].append(self.send(p, 11 + h, half, half, ring(self.me, d2, k)))
        for p in range(3):
            d0, d1, d2 = ORDERS[p]
            for k, h in ((1, 0), (3, 1)):
                self.got[p][k, 1 - h].wait_recv()
                at = ring(self.me, d2, 4 - k)
                self.mate(p, 13 + h, view(self.g, self.dims, self.me, {d0: ALL, d1: ALL}, COLS[p], at))

    def last(self):
        for p in range(3):
            d0, d1, d2 = ORDERS[p]
            for h in range(2):
                self.over[p][h].wait_recv()
            at = ring(self.me, d2, 2)
            self.mate(p, 15, view(self.g, self.dims, self.me, {d0: ALL, d1: ALL}, COLS[p], at))

    def arrive(self):
        for cp in self.mates:
            cp.wait_recv()

    def drain(self):
        for cp in self.sends:
            cp.wait_send()


def plan(meta_row, base):
    slot = lax.broadcasted_iota(jnp.int32, (128, 256), 0).astype(jnp.float32)
    src = (lax.broadcasted_iota(jnp.int32, (1, 256), 1) // 64).astype(jnp.float32) * 32.0
    hot = jnp.zeros((128, 256), jnp.float32)
    gates = jnp.zeros((128, 256), jnp.float32)
    for k in range(4):
        key = meta_row[k : k + 1] - base
        key = jnp.where((key >= 0.0) & (key < 32.0), key + src, -1.0)
        eq = slot == key
        hot += jnp.where(eq, 1.0, 0.0)
        gates += jnp.where(eq, meta_row[4 + k : 5 + k], 0.0)
    return hot.astype(jnp.bfloat16), jnp.sum(gates, axis=1, keepdims=True)


def copy(src, dst, sem):
    cp = pltpu.make_async_copy(src, dst, sem)
    cp.start()
    return cp


def dot(a, b, ca, cb):
    return lax.dot_general(a, b, (((ca,), (cb,)), ((), ())), preferred_element_type=jnp.float32)


BACK = (("z", "y", "x"), ("x", "z", "y"), ("y", "x", "z"))
DEST = ("x", "y", "z")
VOC = 1571
BLOCKS = ((0, 528), (528, 528), (1056, 515))


def routing(ids, proj, tok, odd):
    scores = dot(proj, tok, 1, 1)
    expert = lax.broadcasted_iota(jnp.int32, (EX, 128), 0)
    hot = [(expert == ids[k : k + 1]).astype(jnp.float32) for k in range(4)]
    picked = [jnp.sum(h * scores, axis=0, keepdims=True) for h in hot]
    top = jnp.maximum(jnp.maximum(picked[0], picked[1]), jnp.maximum(picked[2], picked[3]))
    weights = [jnp.exp(p - top) for p in picked]
    total = weights[0] + weights[1] + weights[2] + weights[3]
    a = lax.broadcasted_iota(jnp.int32, (128, 128), 0)
    b = lax.broadcasted_iota(jnp.int32, (128, 128), 1)
    before = ((a < 64) & (a < lax.rem(b, 64))).astype(jnp.bfloat16)
    named = hot[0] + hot[1] + hot[2] + hot[3]
    earlier = dot(named.astype(jnp.bfloat16), before, 1, 0)
    lane = lax.broadcasted_iota(jnp.int32, (1, 128), 1)
    here = lax.div(lane, 64) == odd
    rows = []
    for k in range(4):
        slot = jnp.sum(hot[k] * earlier, axis=0, keepdims=True)
        rows.append(jnp.where(here, ids[k : k + 1].astype(jnp.float32) * SLOTS + slot, 0.0))
    for k in range(4):
        rows.append(jnp.where(here, weights[k] / total, 0.0))
    return rows


def main_kernel(
    t_ref, a_ref, id_ref, pj_ref, heat_ref, wg_ref, wu_ref, wd_ref, emb_ref,
    sc_ref, st_ref, moe_ref, ag_ref, tg_ref,
    wg, wu, wraw, wd, mine, mg, rows, xs, act, hots, gates, tok2,
    emb, lg, to_mate, from_mate, own, in1, sum1, out2, in2, sum2, out3, in3, mb, sb,
    ts, tr, as_, ar, ms, mr, loc, rawsem, toksem, esem, xsem, lsem,
    hs, hr, s1, r1, s2, r2, s3, r3, ssem, rsem,
):
    c = lax.axis_index("c")
    load = [copy(t_ref, tok2.at[pl.ds(64 * h, 64)], loc.at[2 + h]) for h in range(2)]
    me = greet()
    sends = []
    v = me["x"] * 2 + me["c"]
    mate = {"c": 1 - me["c"]}
    tok = Gather(t_ref.at[pl.ds(pl.multiple_of(v * 8, 8), 8)], tg_ref, ("y", "z", "x", "c"), me, ts, tr, loc.at[0])
    tok.first()
    lead = Gather(a_ref, ag_ref, AXES, me, as_, ar, loc.at[1])
    lead.first()
    raw = copy(wd_ref, wraw, rawsem.at[0])
    for cp in load:
        cp.wait()
    made = routing(id_ref[...], pj_ref[...], tok2[...], lax.rem(me["z"], 2))
    for k in range(8):
        mine[pl.ds(k, 1), :] = made[k]
        mg[me["y"], me["z"], pl.ds(k, 1), :] = made[k]
    here = mg.at[me["y"], me["z"]]
    mgot = [remote(mine, here, ms.at[k], mr.at[k], ring(me, "z", k + 1), sends) for k in range(3)]
    tok.second()
    eload = copy(emb_ref, emb, esem)
    raw.wait()

    def low(i, _):
        r = wraw[pl.ds(i * 4, 4)].reshape(16, 2880)
        for v in range(8):
            at = pl.ds(pl.multiple_of(i * 16, 16), 16)
            wd[v % 2, at, pl.ds((v // 2) * 384, 360)] = r[:, 360 * v : 360 * v + 360]
            wd[v % 2, at, pl.ds((v // 2) * 384 + 360, 24)] = jnp.zeros((16, 24), jnp.bfloat16)
        return 0

    lax.fori_loop(0, 45, low, 0)
    raw = copy(wg_ref, wraw, rawsem.at[1])
    for cp in mgot:
        cp.wait_recv()
    row = mg.at[me["y"]]
    mgot = [remote(row, row, ms.at[3 + k], mr.at[3 + k], ring(me, "y", k + 1), sends) for k in range(3)]
    tok.third()
    lead.second()
    raw.wait()

    def flat(dst):
        def body(i, _):
            dst[pl.ds(pl.multiple_of(i * 16, 16), 16), :] = wraw[pl.ds(i * 4, 4)].reshape(16, 2880)
            return 0

        lax.fori_loop(0, 45, body, 0)

    flat(wg)
    raw = copy(wu_ref, wraw, rawsem.at[2])
    tok.forward()
    lead.third()
    raw.wait()
    flat(wu)
    for cp in mgot:
        cp.wait_recv()
    base = ((me["y"] * 4 + me["z"]) * 32).astype(jnp.float32)
    for g in range(4):
        row = jnp.concatenate([mg[g, 0] + mg[g, 1], mg[g, 2] + mg[g, 3]], axis=1)
        hot, gate = plan(row, base)
        hots[g] = hot
        gates[pl.ds(128 * g, 128), :] = jnp.broadcast_to(gate, (128, 128))
    tok.last()
    tok.arrive()
    flat_tok = tg_ref.reshape(1024, 2880)
    loads = [copy(flat_tok.at[pl.ds(256 * g, 256)], rows.at[g], toksem.at[g]) for g in range(2)]
    for g in range(4):
        loads[g].wait()
        xs[pl.ds(128 * g, 128), :] = dot(hots[g], rows[g % 2], 1, 0).astype(jnp.bfloat16)
        if g < 2:
            loads.append(copy(flat_tok.at[pl.ds(256 * (g + 2), 256)], rows.at[g], toksem.at[g + 2]))
    lead.forward()
    for n0, n in ((0, 256), (256, 256), (512, 208)):
        gp = dot(xs[...], wg[pl.ds(n0, n), :], 1, 1)
        up = dot(xs[...], wu[pl.ds(n0, n), :], 1, 1)
        r = lax.broadcasted_iota(jnp.int32, (512, n), 0)
        q = lax.broadcasted_iota(jnp.int32, (512, n), 1)
        keep = lax.rem(lax.div(r, 8), 4) == lax.rem(q, 4)
        h = gp * jax.nn.sigmoid(1.702 * gp) * (up + 1.0)
        act[:, pl.ds(n0, n)] = jnp.where(keep, h, 0.0).astype(jnp.bfloat16)
    lead.last()

    hgot = []
    for half in range(2):
        side = 1 - c if half == 0 else c
        for xx in range(2):
            ys = dot(act[...], wd[side, :, pl.ds(768 * xx, 768)], 1, 0)
            for g in range(4):
                y = ys[128 * g : 128 * (g + 1)] * gates[pl.ds(128 * g, 128), pl.ds(0, 1)]
                high = y.astype(jnp.bfloat16)
                rest = (y - high.astype(jnp.float32)).astype(jnp.bfloat16)
                hot = hots[g]
                mix = dot(jnp.concatenate([hot, hot], axis=0), jnp.concatenate([high, rest], axis=0), 0, 0)
                for x in range(2):
                    for p in range(3):
                        piece = mix[:, 384 * x + 128 * p : 384 * x + 128 * (p + 1)].reshape(4, 64, 128)
                        if half == 0:
                            to_mate[p, 2 * xx + x, g] = piece.astype(jnp.bfloat16)
                        else:
                            own[p, 2 * xx + x, g] = piece
            if half == 0:
                part = pl.ds(2 * xx, 2)
                hgot.append(remote(to_mate.at[:, part], from_mate.at[:, part], hs.at[xx], hr.at[xx], mate, []))
    for cp in hgot:
        cp.wait()

    def index(p, at, full):
        return (p,) + tuple(at[d] if d in at else pl.ds(0, 4) for d in full)

    got1 = []
    for k in (1, 3, 2):
        for p in range(3):
            d = BACK[p][0]
            i = index(p, ring(me, d, k), DEST)
            to_mate[i] = (own[i] + from_mate[i].astype(jnp.float32)).astype(jnp.bfloat16)
            src = to_mate.at[i]
            got1.append((p, k, remote(src, in1.at[p, k - 1], s1.at[p, k - 1], r1.at[p, k - 1], ring(me, d, k), sends)))
    for p in range(3):
        i = index(p, {BACK[p][0]: me[BACK[p][0]]}, DEST)
        sum1[p] = own[i] + from_mate[i].astype(jnp.float32)

    lead.arrive()
    flat_rows = ag_ref.reshape(1024, 2880)
    xload = [copy(flat_rows.at[pl.ds(256 * i, 256)], rows.at[i], xsem.at[i]) for i in range(2)]
    eload.wait()
    stores = []

    def logits(j):
        xload[j].wait()
        inv = 1.0 / (0.5 + 0.25 * heat_ref[:, pl.ds(256 * j, 256)].astype(jnp.float32))
        if j >= 2:
            stores[j - 2].wait()
        buf = lg.at[j % 2]
        top = jnp.full((1, 256), -jnp.inf, jnp.float32)
        for i0, n in BLOCKS:
            r = dot(emb[pl.ds(i0, n), :], rows[j % 2], 1, 1) * inv
            buf[pl.ds(i0, n), :] = r
            top = jnp.maximum(top, jnp.max(r, axis=0, keepdims=True))
        if j < 2:
            xload.append(copy(flat_rows.at[pl.ds(256 * (j + 2), 256)], rows.at[j], xsem.at[j + 2]))

        def tail(i, s):
            return s + jnp.sum(jnp.exp(buf[pl.ds(pl.multiple_of(i * 112, 8), 112), :] - top), axis=0, keepdims=True)

        total = lax.fori_loop(0, 14, tail, jnp.zeros((1, 256), jnp.float32))
        total += jnp.sum(jnp.exp(buf[pl.ds(1568, 3), :] - top), axis=0, keepdims=True)
        for h in range(2):
            mb[0, 0, pl.ds(2 * j + h, 1), :] = top[:, 128 * h : 128 * (h + 1)]
            sb[0, 0, pl.ds(2 * j + h, 1), :] = total[:, 128 * h : 128 * (h + 1)]
        stores.append(copy(buf, sc_ref.at[:, pl.ds(256 * j, 256)], lsem.at[j]))

    stages = [[mate]] + [[ring(me, a, k) for k in range(1, 4)] for a in DEST]

    def begin(i):
        got = []
        for k, dev in enumerate(stages[i]):
            got.append(remote(mb.at[i, 0], mb.at[i, k + 1], ssem.at[0, i, k], rsem.at[0, i, k], dev, sends))
            got.append(remote(sb.at[i, 0], sb.at[i, k + 1], ssem.at[1, i, k], rsem.at[1, i, k], dev, sends))
        return got

    def end(i, got):
        for cp in got:
            cp.wait_recv()
        n = len(stages[i]) + 1
        top = mb[i, 0]
        for k in range(1, n):
            top = jnp.maximum(top, mb[i, k])
        total = sb[i, 0] * jnp.exp(mb[i, 0] - top)
        for k in range(1, n):
            total += sb[i, k] * jnp.exp(mb[i, k] - top)
        if i < 3:
            mb[i + 1, 0] = top
            sb[i + 1, 0] = total
        else:
            st_ref[...] = top + jnp.log(total)

    for j in range(3):
        logits(j)
    for p, k, cp in got1:
        cp.wait_recv()
        sum1[p] += in1[p, k - 1].astype(jnp.float32)
    got2 = []
    for p in range(3):
        d = BACK[p][1]
        first = [a for a in DEST if a != BACK[p][0]]
        for k in (1, 3, 2):
            i = index(p, ring(me, d, k), first)
            out2[p, k - 1] = sum1[i].astype(jnp.bfloat16)
            got2.append((p, k, remote(out2.at[p, k - 1], in2.at[p, k - 1], s2.at[p, k - 1], r2.at[p, k - 1], ring(me, d, k), sends)))
        sum2[p] = sum1[index(p, {d: me[d]}, first)]
    logits(3)
    got = begin(0)
    for p, k, cp in got2:
        cp.wait_recv()
        sum2[p] += in2[p, k - 1].astype(jnp.float32)
    got3 = []
    for p in range(3):
        d = BACK[p][2]
        for k in (1, 3, 2):
            out3[p, k - 1] = sum2[p, lax.rem(me[d] + k, 4)]
            got3.append(remote(out3.at[p, k - 1], in3.at[p, k - 1], s3.at[p, k - 1], r3.at[p, k - 1], ring(me, d, k), sends))
    end(0, got)
    got = begin(1)
    end(1, got)
    got = begin(2)
    for cp in got3:
        cp.wait_recv()
    for p in range(3):
        total = sum2[p, me[BACK[p][2]]]
        for k in range(3):
            total += in3[p, k]
        n = 128 if p < 2 else 104
        moe_ref[:, pl.ds(128 * p, n)] = total[:, :n].astype(jnp.bfloat16)
    end(2, got)
    got = begin(3)
    stores[2].wait()
    stores[3].wait()
    tok.drain()
    lead.drain()
    for cp in sends[: -len(got)]:
        cp.wait_send()
    end(3, got)
    for cp in got:
        cp.wait_send()


def main(tok, lead, ids, proj, heat, w_gate, w_up, w_down, embed):
    bf, f32 = jnp.bfloat16, jnp.float32
    dma = pltpu.SemaphoreType.DMA
    hbm = pl.BlockSpec(memory_space=pl.ANY)
    vm = pl.BlockSpec(memory_space=pltpu.VMEM)
    V = pltpu.VMEM
    return pl.pallas_call(
        main_kernel,
        out_shape=(
            jax.ShapeDtypeStruct((VOC, 1024), f32), jax.ShapeDtypeStruct((8, 128), f32),
            jax.ShapeDtypeStruct((64, 360), bf),
            jax.ShapeDtypeStruct((4, 2, 4, 4, 8, 2880), bf), jax.ShapeDtypeStruct((4, 4, 4, 2, 8, 2880), bf),
        ),
        in_specs=[hbm, hbm, vm, vm, vm, hbm, hbm, hbm, hbm],
        out_specs=[hbm, vm, vm, hbm, hbm],
        scratch_shapes=[
            V((720, 2880), bf), V((720, 2880), bf), V((180, 4, 2880), bf), V((2, 720, 1536), bf),
            V((8, 128), f32), V((4, 4, 8, 128), f32), V((2, 256, 2880), bf), V((512, 2880), bf), V((512, 720), bf),
            V((4, 128, 256), bf), V((512, 128), f32), V((128, 2880), bf),
            V((VOC, 2880), bf), V((2, VOC, 256), f32),
            V((3, 4, 4, 4, 64, 128), bf), V((3, 4, 4, 4, 64, 128), bf), V((3, 4, 4, 4, 64, 128), f32),
            V((3, 3, 4, 4, 64, 128), bf), V((3, 4, 4, 64, 128), f32),
            V((3, 3, 4, 64, 128), bf), V((3, 3, 4, 64, 128), bf), V((3, 4, 64, 128), f32),
            V((3, 3, 64, 128), f32), V((3, 3, 64, 128), f32),
            V((4, 4, 8, 128), f32), V((4, 4, 8, 128), f32),
        ]
        + [dma((3, 16))] * 4 + [dma((6,))] * 2 + [dma((4,)), dma((3,)), dma((4,)), dma, dma((4,)), dma((4,))]
        + [dma((2,))] * 2 + [dma((3, 3))] * 6 + [dma((2, 4, 3))] * 2,
        compiler_params=pltpu.CompilerParams(collective_id=0, has_side_effects=True, vmem_limit_bytes=67043328),
    )(tok, lead, ids, proj, heat, w_gate, w_up, w_down, embed)


STEPS = tuple((200 * i, 200 if i < 7 else 171) for i in range(8))


def last_kernel(s_ref, t_ref, o_ref, buf, isem, osem):
    loads = [copy(s_ref.at[pl.ds(i0, n)], buf.at[pl.ds(i0, n)], isem.at[i]) for i, (i0, n) in enumerate(STEPS)]
    outs = []
    for i, (i0, n) in enumerate(STEPS):
        loads[i].wait()
        buf[pl.ds(i0, n), :] = buf[pl.ds(i0, n), :] - t_ref[...]
        outs.append(copy(buf.at[pl.ds(i0, n)], o_ref.at[pl.ds(i0, n)], osem.at[i]))
    for cp in outs:
        cp.wait()


def last(scaled, shift):
    hbm = pl.BlockSpec(memory_space=pl.ANY)
    dma = pltpu.SemaphoreType.DMA
    return pl.pallas_call(
        last_kernel, out_shape=jax.ShapeDtypeStruct((VOC, 1024), jnp.float32),
        in_specs=[hbm, pl.BlockSpec(memory_space=pltpu.VMEM)], out_specs=hbm,
        scratch_shapes=[pltpu.VMEM((VOC, 1024), jnp.float32), dma((8,)), dma((8,))],
    )(scaled, shift)


def per_device(lead, heat, embed, tok, choice, proj, w_gate, w_up, w_down):
    flip = lambda w: jnp.transpose(w, (2, 0, 1))
    ids = choice.T
    scaled, shift, moe, _, _ = main(
        tok, lead, jnp.concatenate([ids, ids], axis=1), proj.T, heat.reshape(1, 1024),
        flip(w_gate), flip(w_up), jnp.transpose(w_down, (1, 0, 2)), embed,
    )
    return last(scaled, shift.reshape(1, 1024)).T, moe


def solution(mesh):
    torus = Mesh(mesh.devices.reshape(4, 2, 4, 4), AXES)
    placed = (
        P(AXES, None), P(), P(AXES, None), P(EXPERT, None), P(EXPERT, None), P(),
        P(EXPERT, None, VOCAB), P(EXPERT, None, VOCAB), P(EXPERT, VOCAB, None),
    )
    return jax.shard_map(
        per_device, mesh=torus, in_specs=placed,
        out_specs=(P(None, AXES), P(EXPERT, VOCAB)), check_vma=False,
    )
```

time: 113 us -> 94.9 us (0.84)
  Pallas kernels: 105 us -> 91.9 us
  other arithmetic: 4.19 us -> 1.41 us
  matrix products: 1.38 us -> 0 us
    pallas_call x3 -> x2, Pallas kernels: 105 us -> 91.9 us  [the longest x1 85.6 us: main(): pl.pallas_call(main_kernel, out_shape=(jax.ShapeDtypeStruct((VOC, 1024),...]
    reduce_sum x3 -> x0, other arithmetic: 1.46 us -> none  [the longest x1 0.73 us: routing(): slots = jnp.sum(hot * earlier[None], axis=1)]
    dot_general x2 -> x0, matrix products: 1.38 us -> none  [the longest x1 1.25 us: routing(): lax.dot_general(proj, tok, (((0,), (1,)), ((), ())), preferred_element_ty...]
    div x1 -> x0, other arithmetic: 1.33 us -> none  [per_device(): inv_temp = (1.0 / (0.5 + 0.25 * heat.astype(jnp.float32))).reshape(1, 1024)]
where the time goes in v3:
time: 94.9 us; the launch traced here: 94.6 us
  Pallas kernels  91.9 us (97%)
  other arithmetic  1.41 us (1%)
    pallas_call x1, Pallas kernels, main(): pl.pallas_call(main_kernel, out_shape=(jax.ShapeDtypeStruct((VOC, 1024),...  85.6 us
    pallas_call x1, Pallas kernels, last(): pl.pallas_call(last_kernel, out_shape=jax.ShapeDtypeStruct((VOC, 1024), j...  6.34 us

profile of v3, /device:TPU:0, one launch (start us, length us, event | category | flops | bytes accessed | tf_op | source)
XLA Modules:
  0.0 94.6 jit_solution(2772441060584705149)
XLA Ops:
  0.6 1.4 %pad_add_fusion.id_ref = s32[4,128]{1,0:T(4,128)} fusion(s32[4,64]{1,0:T(4,128)} %bitcast.15), kind=kLoop, calls=%fused_computation | loop fusion | flops 512 | bytes 3072 | tf_op jit(solution)/shard_map/concatenate | solution.py:477
  2.0 85.6 %shard_map.104 = (f32[1571,1024]{1,0:T(8,128)}, f32[8,128]{1,0:T(8,128)}, bf16[64,360]{1,0:T(8,128)(2,1)}, bf16[4,2,4,4,8,2880]{5,4,3,2,1,0:T(8,128)(2,1)}, bf16[4,4,4,2,8,2880]{5,4,3,2,1,0:T(8,128)(2,1)}) custom-call(bf16[64,2880]{1,0:T(8,128)(2,1)} %t_ref.1, bf16[8,2880]{1,0:T(8,128)(2,1)} %a_ref.1, s32[4,128]{1,0:T(4,128)} %pad_add_fusion.id_ref, ...), custom_call_target="tpu_custom_call" | custom-call | tf_op jit(solution)/shard_map/pallas_call | solution.py:423
  87.6 0.0 copy-start
  87.6 6.3 %shard_map.105 = f32[1571,1024]{1,0:T(8,128)} custom-call(f32[1571,1024]{1,0:T(8,128)} %get-tuple-element.5.s_ref, f32[1,1024]{1,0:T(1,128)} %bitcast.13), custom_call_target="tpu_custom_call" | custom-call | tf_op jit(solution)/shard_map/pallas_call | solution.py:466
  94.0 0.0 copy-done
  94.0 0.6 copy.12
Async XLA Ops:
  87.6 6.4 %copy-start = (bf16[64,360]{1,0:T(8,128)(2,1)S(1)}, bf16[64,360]{1,0:T(8,128)(2,1)}, u32[]{:S(2)}) copy-start(bf16[64,360]{1,0:T(8,128)(2,1)} %get-tuple-element.11) | copy-start | bytes 138244

commit v4 on v3

v4 whole, which is shorter than its diff:
```python
import functools

import jax
import jax.numpy as jnp
from jax import lax
from jax.experimental import pallas as pl
from jax.experimental.pallas import tpu as pltpu
from jax.sharding import Mesh
from jax.sharding import PartitionSpec as P

AXES = ("x", "c", "y", "z")
EXPERT = ("y", "z")
VOCAB = ("x", "c")
MESH = pl.DeviceIdType.MESH
COLS = ((0, 1024), (1024, 1024), (2048, 832))
TCOLS = ((0, 640), (640, 1152), (1792, 1088))
ORDERS = (("z", "y", "x"), ("x", "z", "y"), ("x", "y", "z"))
EX, HOLD, SLOTS = 64, 4, 8


def ring(me, axis, step):
    return {axis: lax.rem(me[axis] + step, 4)}


def greet():
    me = {a: lax.axis_index(a) for a in AXES}
    barrier = pltpu.get_barrier_semaphore()
    for a in ("x", "y", "z"):
        for k in range(1, 4):
            pl.semaphore_signal(barrier, inc=1, device_id=ring(me, a, k), device_id_type=MESH)
    pl.semaphore_signal(barrier, inc=1, device_id={"c": 1 - me["c"]}, device_id_type=MESH)
    return me, barrier


def view(g, dims, me, ranges, cols, at={}):
    idx = [ranges.get(a, at.get(a, me[a])) for a in dims]
    return g.at[idx[0], idx[1], idx[2], idx[3], :, pl.ds(*cols)]


def remote(src, dst, ssem, rsem, dev, sends):
    cp = pltpu.make_async_remote_copy(
        src_ref=src, dst_ref=dst, send_sem=ssem, recv_sem=rsem, device_id=dev, device_id_type=MESH
    )
    cp.start()
    sends.append(cp)
    return cp


ALL = pl.ds(0, 4)


class Gather:
    def __init__(self, a, g, dims, cols, shared, me, ssem, rsem, own):
        self.dims, self.cols, self.shared = dims, cols, shared
        self.orders = ORDERS if shared else BACK
        self.a, self.g, self.me, self.ssem, self.rsem = a, g, me, ssem, rsem
        self.sends, self.mates, self.got, self.over = [], [], [None] * 3, [None] * 3
        x, c, y, z = (me[d] for d in AXES)
        if shared:
            n = cols[0][1]
            left, right = pl.ds(0, n), pl.ds(n, 2880 - n)
            self.own = [
                copy(a.at[x, c, :, left], g.at[y, z, x, c, :, left], own[0]),
                copy(a.at[:, c, :, right], g.at[y, z, :, c, :, right], own[1]),
            ]
        else:
            self.own = [copy(a, g.at[x, c, y, z], own[0])]

    def settle(self):
        for cp in self.own:
            cp.wait()

    def send(self, p, k, src, dst, dev):
        return remote(src, dst, self.ssem.at[p, k], self.rsem.at[p, k], dev, self.sends)

    def view(self, p, ranges, at={}):
        return view(self.g, self.dims, self.me, ranges, self.cols[p], at)

    def skips(self, p):
        return self.shared and self.orders[p][0] == "x"

    def first(self):
        me = self.me
        for p in range(3):
            d0, d1, _ = self.orders[p]
            if self.skips(p):
                src = self.a.at[:, me["c"], :, pl.ds(*self.cols[p])]
                dst = self.view(p, {d0: ALL})
                self.got[p] = [self.send(p, 2 + k, src, dst, ring(me, d1, k)) for k in (1, 3, 2)]
            else:
                src = self.a.at[me["x"], me["c"]] if self.shared else self.a
                src = src.at[:, pl.ds(*self.cols[p])]
                self.got[p] = [self.send(p, k - 1, src, self.view(p, {}), ring(me, d0, k)) for k in (1, 3, 2)]

    def second(self, p):
        for cp in self.got[p]:
            cp.wait_recv()
        d0, d1, _ = self.orders[p]
        blk = self.view(p, {d0: ALL})
        self.got[p] = [self.send(p, 2 + k, blk, blk, ring(self.me, d1, k)) for k in (1, 3, 2)]

    def mate(self, p, k, blk):
        self.mates.append(self.send(p, k, blk, blk, {"c": 1 - self.me["c"]}))

    def third(self, p):
        for cp in self.got[p]:
            cp.wait_recv()
        d0, d1, d2 = self.orders[p]
        halves = [self.view(p, {d0: pl.ds(2 * h, 2), d1: ALL}) for h in range(2)]
        self.got[p] = {}
        for o in range(2):
            for k, h in ((1, o), (3, 1 - o)):
                self.got[p][k, h] = self.send(p, 6 + 2 * (k // 2) + h, halves[h], halves[h], ring(self.me, d2, k))
        self.mate(p, 10, self.view(p, {d0: ALL, d1: ALL}))

    def forward(self, parts=(0, 1, 2)):
        for p in parts:
            d0, d1, d2 = self.orders[p]
            self.over[p] = []
            for k, h in ((1, 0), (3, 1)):
                self.got[p][k, h].wait_recv()
                half = self.view(p, {d0: pl.ds(2 * h, 2), d1: ALL}, ring(self.me, d2, 4 - k))
                self.over[p].append(self.send(p, 11 + h, half, half, ring(self.me, d2, k)))
        for p in parts:
            d0, d1, d2 = self.orders[p]
            for k, h in ((1, 0), (3, 1)):
                self.got[p][k, 1 - h].wait_recv()
                self.mate(p, 13 + h, self.view(p, {d0: ALL, d1: ALL}, ring(self.me, d2, 4 - k)))

    def last(self, parts=(0, 1, 2)):
        for p in parts:
            d0, d1, d2 = self.orders[p]
            for h in range(2):
                self.over[p][h].wait_recv()
            self.mate(p, 15, self.view(p, {d0: ALL, d1: ALL}, ring(self.me, d2, 2)))

    def arrive(self):
        for cp in self.mates:
            cp.wait_recv()

    def drain(self):
        for cp in self.sends:
            cp.wait_send()


def plan(meta_row, base):
    slot = lax.broadcasted_iota(jnp.int32, (128, 256), 0).astype(jnp.float32)
    src = (lax.broadcasted_iota(jnp.int32, (1, 256), 1) // 64).astype(jnp.float32) * 32.0
    hot = jnp.zeros((128, 256), jnp.float32)
    gates = jnp.zeros((128, 256), jnp.float32)
    for k in range(4):
        key = meta_row[k : k + 1] - base
        key = jnp.where((key >= 0.0) & (key < 32.0), key + src, -1.0)
        eq = slot == key
        hot += jnp.where(eq, 1.0, 0.0)
        gates += jnp.where(eq, meta_row[4 + k : 5 + k], 0.0)
    return hot.astype(jnp.bfloat16), jnp.sum(gates, axis=1, keepdims=True)


def copy(src, dst, sem):
    cp = pltpu.make_async_copy(src, dst, sem)
    cp.start()
    return cp


def dot(a, b, ca, cb):
    return lax.dot_general(a, b, (((ca,), (cb,)), ((), ())), preferred_element_type=jnp.float32)


BACK = (("z", "y", "x"), ("x", "z", "y"), ("y", "x", "z"))
DEST = ("x", "y", "z")
VOC = 1571
VMEM_LIMIT = 67043328
BLOCKS = ((0, 528), (528, 528), (1056, 515))


def routing(ids, proj, tok, odd):
    scores = dot(proj, tok, 1, 1)
    twice = lax.broadcasted_iota(jnp.int32, (64, 128), 0) == lax.rem(lax.broadcasted_iota(jnp.int32, (64, 128), 1), 64)
    ids = dot(ids.astype(jnp.float32).astype(jnp.bfloat16), twice.astype(jnp.float32).astype(jnp.bfloat16), 1, 0)
    expert = lax.broadcasted_iota(jnp.int32, (EX, 128), 0).astype(jnp.float32)
    hot = [(expert == ids[k : k + 1]).astype(jnp.float32) for k in range(4)]
    picked = [jnp.sum(h * scores, axis=0, keepdims=True) for h in hot]
    top = jnp.maximum(jnp.maximum(picked[0], picked[1]), jnp.maximum(picked[2], picked[3]))
    weights = [jnp.exp(p - top) for p in picked]
    total = weights[0] + weights[1] + weights[2] + weights[3]
    a = lax.broadcasted_iota(jnp.int32, (128, 128), 0)
    b = lax.broadcasted_iota(jnp.int32, (128, 128), 1)
    before = ((a < 64) & (a < lax.rem(b, 64))).astype(jnp.bfloat16)
    named = hot[0] + hot[1] + hot[2] + hot[3]
    earlier = dot(named.astype(jnp.bfloat16), before, 1, 0)
    lane = lax.broadcasted_iota(jnp.int32, (1, 128), 1)
    here = lax.div(lane, 64) == odd
    rows = []
    for k in range(4):
        slot = jnp.sum(hot[k] * earlier, axis=0, keepdims=True)
        rows.append(jnp.where(here, ids[k : k + 1] * SLOTS + slot, 0.0))
    for k in range(4):
        rows.append(jnp.where(here, weights[k] / total, 0.0))
    return rows


def main_kernel(
    t_ref, a_ref, id_ref, pj_ref, heat_ref, wg_ref, wu_ref, wd_ref, emb_ref,
    sc_ref, st_ref, moe_ref, ag_ref,
    stv, moev, tg, wg, wu, wraw, wd, mine, mg, rows, xs, act, hots, gates, tok2,
    emb, lg, to_mate, from_mate, own, in1, sum1, out2, in2, sum2, out3, in3, mb, sb,
    ts, tr, as_, ar, ms, mr, loc, rawsem, esem, xsem, lsem, osem,
    hs, hr, s1, r1, s2, r2, s3, r3, ssem, rsem,
):
    c = lax.axis_index("c")
    load = [copy(t_ref, tok2.at[pl.ds(64 * h, 64)], loc.at[2 + h]) for h in range(2)]
    chunks = [(w, i) for w in (wd_ref, wg_ref, wu_ref) for i in range(5)]
    raws = []

    def fetch(n):
        w, i = chunks[n]
        raws.append(copy(w.at[pl.ds(36 * i, 36)], wraw.at[n % 2], rawsem.at[n]))

    fetch(0)
    fetch(1)
    me, barrier = greet()
    for cp in load:
        cp.wait()
    made = routing(id_ref[...], pj_ref[...], tok2[...], lax.rem(me["z"], 2))
    for k in range(8):
        mine[pl.ds(k, 1), :] = made[k]
        mg[me["y"], me["z"], pl.ds(k, 1), :] = made[k]
    pl.semaphore_wait(barrier, 10)
    sends = []
    mate = {"c": 1 - me["c"]}
    here = mg.at[me["y"], me["z"]]
    mgot = [remote(mine, here, ms.at[k], mr.at[k], ring(me, "z", k + 1), sends) for k in range(3)]
    tok = Gather(t_ref.reshape(4, 2, 8, 2880), tg, ("y", "z", "x", "c"), TCOLS, True, me, ts, tr, (loc.at[0], loc.at[4]))
    tok.first()
    lead = Gather(a_ref, ag_ref, AXES, COLS, False, me, as_, ar, (loc.at[1],))
    lead.first()

    def relay(n):
        w, c0 = n // 5, 144 * (n % 5)
        raws[n].wait()

        def body(i, _):
            r = wraw[n % 2, pl.ds(i * 4, 4)].reshape(16, 2880)
            at = pl.ds(pl.multiple_of(c0 + i * 16, 16), 16)
            if w > 0:
                (wg, wu)[w - 1][at, :] = r
                return 0
            for v in range(8):
                wd[v % 2, at, pl.ds((v // 2) * 384, 360)] = r[:, 360 * v : 360 * v + 360]
                wd[v % 2, at, pl.ds((v // 2) * 384 + 360, 24)] = jnp.zeros((16, 24), jnp.bfloat16)
            return 0

        lax.fori_loop(0, 9, body, 0)
        if n + 2 < 15:
            fetch(n + 2)

    for n in range(2):
        relay(n)
    tok.settle()
    for cp in mgot:
        cp.wait_recv()
    row = mg.at[me["y"]]
    mgot = [remote(row, row, ms.at[3 + k], mr.at[3 + k], ring(me, "y", k + 1), sends) for k in range(3)]
    tok.second(0)
    tok.third(1)
    tok.third(2)
    lead.settle()
    for p in range(3):
        lead.second(p)
    for n in range(2, 4):
        relay(n)
    eload = copy(emb_ref, emb, esem)
    for n in range(4, 6):
        relay(n)
    tok.third(0)
    for n in range(6, 9):
        relay(n)
    tok.forward((1, 2))
    for n in range(9, 12):
        relay(n)
    tok.forward((0,))
    for p in range(3):
        lead.third(p)
    for n in range(12, 15):
        relay(n)
    for cp in mgot:
        cp.wait_recv()
    base = ((me["y"] * 4 + me["z"]) * 32).astype(jnp.float32)
    for g in range(4):
        row = jnp.concatenate([mg[g, 0] + mg[g, 1], mg[g, 2] + mg[g, 3]], axis=1)
        hot, gate = plan(row, base)
        hots[g] = hot
        gates[pl.ds(128 * g, 128), :] = jnp.broadcast_to(gate, (128, 128))
    tok.last((1, 2, 0))
    tok.arrive()
    tokens = tg.reshape(1024, 2880)
    for g in range(4):
        xs[pl.ds(128 * g, 128), :] = dot(hots[g], tokens[pl.ds(256 * g, 256), :], 1, 0).astype(jnp.bfloat16)
    for n0, n in ((0, 256), (256, 256), (512, 208)):
        gp = dot(xs[...], wg[pl.ds(n0, n), :], 1, 1)
        up = dot(xs[...], wu[pl.ds(n0, n), :], 1, 1)
        r = lax.broadcasted_iota(jnp.int32, (512, n), 0)
        q = lax.broadcasted_iota(jnp.int32, (512, n), 1)
        keep = lax.rem(lax.div(r, 8), 4) == lax.rem(q, 4)
        h = gp * jax.nn.sigmoid(1.702 * gp) * (up + 1.0)
        act[:, pl.ds(n0, n)] = jnp.where(keep, h, 0.0).astype(jnp.bfloat16)
        if n0 == 0:
            lead.forward()

    hgot, xload, stores = [], [], []
    flat_rows = ag_ref.reshape(1024, 2880)
    for half in range(2):
        side = 1 - c if half == 0 else c
        for xx in range(2):
            if half == 0 and xx == 1:
                lead.last()
            if half == 1 and xx == 1:
                lead.arrive()
                xload += [copy(flat_rows.at[pl.ds(256 * i, 256)], rows.at[i], xsem.at[i]) for i in range(2)]
                eload.wait()
            ys = dot(act[...], wd[side, :, pl.ds(768 * xx, 768)], 1, 0)
            for g in range(4):
                y = ys[128 * g : 128 * (g + 1)] * gates[pl.ds(128 * g, 128), pl.ds(0, 1)]
                high = y.astype(jnp.bfloat16)
                rest = (y - high.astype(jnp.float32)).astype(jnp.bfloat16)
                hot = hots[g]
                mix = dot(jnp.concatenate([hot, hot], axis=0), jnp.concatenate([high, rest], axis=0), 0, 0)
                for x in range(2):
                    for p in range(3):
                        piece = mix[:, 384 * x + 128 * p : 384 * x + 128 * (p + 1)].reshape(4, 64, 128)
                        if half == 0:
                            to_mate[p, 2 * xx + x, g] = piece.astype(jnp.bfloat16)
                        else:
                            own[p, 2 * xx + x, g] = piece
            if half == 0:
                part = pl.ds(2 * xx, 2)
                hgot.append(remote(to_mate.at[:, part], from_mate.at[:, part], hs.at[xx], hr.at[xx], mate, []))

    tops, sums = [], []

    def fold(x, f):
        n = x.shape[0] // 8 * 8
        return f(x[:n].reshape(n // 8, 8, x.shape[1]), axis=0)

    def expo(j, i0, n):
        return jnp.exp(lg[j % 2, pl.ds(i0, n), :] - tops[j])

    def logits(j):
        xload[j].wait()
        inv = 1.0 / (0.5 + 0.25 * heat_ref[:, pl.ds(256 * j, 256)].astype(jnp.float32))
        if j >= 2:
            stores[j - 2].wait()
        top = jnp.full((8, 256), -jnp.inf, jnp.float32)
        total = jnp.zeros((8, 256), jnp.float32)
        for i0, n in BLOCKS:
            r = dot(emb[pl.ds(i0, n), :], rows[j % 2], 1, 1) * inv
            lg[j % 2, pl.ds(i0, n), :] = r
            top = jnp.maximum(top, fold(r, jnp.max))
            if j > 0:
                total += fold(expo(j - 1, i0, n // 8 * 8), jnp.sum)
        if j > 0:
            sums.append(jnp.sum(total, axis=0, keepdims=True) + jnp.sum(expo(j - 1, 1568, 3), axis=0, keepdims=True))
        top = jnp.max(top, axis=0, keepdims=True)
        tops.append(jnp.maximum(top, jnp.max(lg[j % 2, pl.ds(1568, 3), :], axis=0, keepdims=True)))
        if j < 2:
            xload.append(copy(flat_rows.at[pl.ds(256 * (j + 2), 256)], rows.at[j], xsem.at[j + 2]))
        stores.append(copy(lg.at[j % 2], sc_ref.at[:, pl.ds(256 * j, 256)], lsem.at[j]))

    def put(j):
        for h in range(2):
            mb[0, 0, pl.ds(2 * j + h, 1), :] = tops[j][:, 128 * h : 128 * (h + 1)]
            sb[0, 0, pl.ds(2 * j + h, 1), :] = sums[j][:, 128 * h : 128 * (h + 1)]

    logits(0)
    for cp in hgot:
        cp.wait()

    def index(p, at, full):
        return (p,) + tuple(at[d] if d in at else pl.ds(0, 4) for d in full)

    got1 = []
    for k in (1, 3, 2):
        for p in range(3):
            d = BACK[p][0]
            i = index(p, ring(me, d, k), DEST)
            to_mate[i] = (own[i] + from_mate[i].astype(jnp.float32)).astype(jnp.bfloat16)
            src = to_mate.at[i]
            got1.append((p, k, remote(src, in1.at[p, k - 1], s1.at[p, k - 1], r1.at[p, k - 1], ring(me, d, k), sends)))
    for p in range(3):
        i = index(p, {BACK[p][0]: me[BACK[p][0]]}, DEST)
        sum1[p] = own[i] + from_mate[i].astype(jnp.float32)

    stages = [[mate]] + [[ring(me, a, k) for k in range(1, 4)] for a in DEST]

    def begin(i):
        got = []
        for k, dev in enumerate(stages[i]):
            got.append(remote(mb.at[i, 0], mb.at[i, k + 1], ssem.at[0, i, k], rsem.at[0, i, k], dev, sends))
            got.append(remote(sb.at[i, 0], sb.at[i, k + 1], ssem.at[1, i, k], rsem.at[1, i, k], dev, sends))
        return got

    def end(i, got):
        for cp in got:
            cp.wait_recv()
        n = len(stages[i]) + 1
        top = mb[i, 0]
        for k in range(1, n):
            top = jnp.maximum(top, mb[i, k])
        total = sb[i, 0] * jnp.exp(mb[i, 0] - top)
        for k in range(1, n):
            total += sb[i, k] * jnp.exp(mb[i, k] - top)
        if i < 3:
            mb[i + 1, 0] = top
            sb[i + 1, 0] = total
        else:
            stv[...] = top + jnp.log(total)

    for j in range(1, 4):
        logits(j)
        put(j - 1)
    total = jnp.zeros((8, 256), jnp.float32)
    for i0, n in BLOCKS:
        total += fold(expo(3, i0, n // 8 * 8), jnp.sum)
    sums.append(jnp.sum(total, axis=0, keepdims=True) + jnp.sum(expo(3, 1568, 3), axis=0, keepdims=True))
    put(3)
    got = begin(0)
    for p, k, cp in got1:
        cp.wait_recv()
        sum1[p] += in1[p, k - 1].astype(jnp.float32)
    rest = [[a for a in DEST if a != BACK[p][0]] for p in range(3)]
    for p in range(3):
        d = BACK[p][1]
        for k in (1, 3, 2):
            out2[p, k - 1] = sum1[index(p, ring(me, d, k), rest[p])].astype(jnp.bfloat16)
        sum2[p] = sum1[index(p, {d: me[d]}, rest[p])]
    end(0, got)
    got = begin(1)
    got2 = [
        (p, k, remote(out2.at[p, k - 1], in2.at[p, k - 1], s2.at[p, k - 1], r2.at[p, k - 1], ring(me, BACK[p][1], k), sends))
        for k in (1, 3, 2)
        for p in range(3)
    ]
    end(1, got)
    got = begin(2)
    for p, k, cp in got2:
        cp.wait_recv()
        sum2[p] += in2[p, k - 1].astype(jnp.float32)
    got3 = []
    for p in range(3):
        d = BACK[p][2]
        for k in (1, 3, 2):
            out3[p, k - 1] = sum2[p, lax.rem(me[d] + k, 4)]
            got3.append(remote(out3.at[p, k - 1], in3.at[p, k - 1], s3.at[p, k - 1], r3.at[p, k - 1], ring(me, d, k), sends))
    end(2, got)
    got = begin(3)
    tok.drain()
    lead.drain()
    for cp in stores[2:]:
        cp.wait()
    for cp in sends[: -len(got)]:
        cp.wait_send()
    for cp in got3:
        cp.wait_recv()
    for p in range(3):
        total = sum2[p, me[BACK[p][2]]]
        for k in range(3):
            total += in3[p, k]
        n = 128 if p < 2 else 104
        moev[:, pl.ds(128 * p, n)] = total[:, :n].astype(jnp.bfloat16)
    moe_out = copy(moev, moe_ref, osem.at[0])
    end(3, got)
    st_out = copy(stv, st_ref, osem.at[1])
    moe_out.wait()
    for cp in got:
        cp.wait_send()
    st_out.wait()


def main(tok, lead, ids, proj, heat, w_gate, w_up, w_down, embed):
    bf, f32 = jnp.bfloat16, jnp.float32
    dma = pltpu.SemaphoreType.DMA
    hbm = pl.BlockSpec(memory_space=pl.ANY)
    vm = pl.BlockSpec(memory_space=pltpu.VMEM)
    V = pltpu.VMEM
    return pl.pallas_call(
        main_kernel,
        out_shape=(
            jax.ShapeDtypeStruct((VOC, 1024), f32), jax.ShapeDtypeStruct((8, 128), f32),
            jax.ShapeDtypeStruct((64, 360), bf),
            jax.ShapeDtypeStruct((4, 2, 4, 4, 8, 2880), bf),
        ),
        in_specs=[hbm, hbm, vm, vm, vm, hbm, hbm, hbm, hbm],
        out_specs=[hbm, hbm, hbm, hbm],
        scratch_shapes=[
            V((8, 128), f32), V((64, 360), bf), V((4, 4, 4, 2, 8, 2880), bf), V((720, 2880), bf), V((720, 2880), bf), V((2, 36, 4, 2880), bf), V((2, 720, 1536), bf),
            V((8, 128), f32), V((4, 4, 8, 128), f32), V((2, 256, 2880), bf), V((512, 2880), bf), V((512, 720), bf),
            V((4, 128, 256), bf), V((512, 128), f32), V((128, 2880), bf),
            V((VOC, 2880), bf), V((2, VOC, 256), f32),
            V((3, 4, 4, 4, 64, 128), bf), V((3, 4, 4, 4, 64, 128), bf), V((3, 4, 4, 4, 64, 128), f32),
            V((3, 3, 4, 4, 64, 128), bf), V((3, 4, 4, 64, 128), f32),
            V((3, 3, 4, 64, 128), bf), V((3, 3, 4, 64, 128), bf), V((3, 4, 64, 128), f32),
            V((3, 3, 64, 128), f32), V((3, 3, 64, 128), f32),
            V((4, 4, 8, 128), f32), V((4, 4, 8, 128), f32),
        ]
        + [dma((3, 16))] * 4 + [dma((6,))] * 2 + [dma((5,)), dma((15,)), dma, dma((4,)), dma((4,)), dma((2,))]
        + [dma((2,))] * 2 + [dma((3, 3))] * 6 + [dma((2, 4, 3))] * 2,
        compiler_params=pltpu.CompilerParams(collective_id=0, has_side_effects=True, vmem_limit_bytes=VMEM_LIMIT),
    )(tok, lead, ids, proj, heat, w_gate, w_up, w_down, embed)


STEPS = tuple((200 * i, 200 if i < 7 else 171) for i in range(8))


def last_kernel(s_ref, t_ref, e_ref, o_ref, eo_ref, buf, ebuf, isem, osem, esem):
    loads = [copy(s_ref.at[pl.ds(i0, n)], buf.at[pl.ds(i0, n)], isem.at[i]) for i, (i0, n) in enumerate(STEPS)]
    small = copy(e_ref, ebuf, esem.at[0])
    outs = []
    for i, (i0, n) in enumerate(STEPS):
        loads[i].wait()
        if i == 4:
            small.wait()
            outs.append(copy(ebuf, eo_ref, esem.at[1]))
        buf[pl.ds(i0, n), :] = buf[pl.ds(i0, n), :] - t_ref[...]
        outs.append(copy(buf.at[pl.ds(i0, n)], o_ref.at[pl.ds(i0, n)], osem.at[i]))
    for cp in outs:
        cp.wait()


def last(scaled, shift, moe):
    hbm = pl.BlockSpec(memory_space=pl.ANY)
    vm = pl.BlockSpec(memory_space=pltpu.VMEM)
    dma = pltpu.SemaphoreType.DMA
    return pl.pallas_call(
        last_kernel, out_shape=(jax.ShapeDtypeStruct((VOC, 1024), jnp.float32), jax.ShapeDtypeStruct((64, 360), jnp.bfloat16)),
        in_specs=[hbm, vm, hbm], out_specs=[hbm, hbm],
        scratch_shapes=[pltpu.VMEM((VOC, 1024), jnp.float32), pltpu.VMEM((64, 360), jnp.bfloat16), dma((8,)), dma((8,)), dma((2,))],
        compiler_params=pltpu.CompilerParams(vmem_limit_bytes=67043328),
    )(scaled, shift, moe)


def per_device(lead, heat, embed, tok, choice, proj, w_gate, w_up, w_down):
    flip = lambda w: jnp.transpose(w, (2, 0, 1))
    scaled, shift, moe, _ = main(
        tok, lead, choice.T, proj.T, heat.reshape(1, 1024),
        flip(w_gate), flip(w_up), jnp.transpose(w_down, (1, 0, 2)), embed,
    )
    out, moe = last(scaled, shift.reshape(1, 1024), moe)
    return out.T, moe


def solution(mesh):
    torus = Mesh(mesh.devices.reshape(4, 2, 4, 4), AXES)
    placed = (
        P(AXES, None), P(), P(AXES, None), P(EXPERT, None), P(EXPERT, None), P(),
        P(EXPERT, None, VOCAB), P(EXPERT, None, VOCAB), P(EXPERT, VOCAB, None),
    )
    return jax.shard_map(
        per_device, mesh=torus, in_specs=placed,
        out_specs=(P(None, AXES), P(EXPERT, VOCAB)), check_vma=False,
    )
```

time: 94.9 us -> 85.6 us (0.902)
  Pallas kernels: 91.9 us -> 84.5 us
  other arithmetic: 1.41 us -> 0 us
    pallas_call x1, Pallas kernels: 85.6 us -> 78.1 us  [main(): pl.pallas_call(main_kernel, out_shape=(jax.ShapeDtypeStruct((VOC, 1024),...]
    concatenate x1 -> x0, other arithmetic: 1.41 us -> none  [per_device(): jnp.concatenate([ids, ids], axis=1)]
where the time goes in v4:
time: 85.6 us; the launch traced here: 85.4 us
  Pallas kernels  84.5 us (99%)
    pallas_call x1, Pallas kernels, main(): pl.pallas_call(main_kernel, out_shape=(jax.ShapeDtypeStruct((VOC, 1024),...  78.1 us
    pallas_call x1, Pallas kernels, last(): pl.pallas_call(last_kernel, out_shape=(jax.ShapeDtypeStruct((VOC, 1024),...  6.46 us

profile of v4, /device:TPU:0, one launch (start us, length us, event | category | flops | bytes accessed | tf_op | source)
XLA Modules:
  0.0 85.4 jit_solution(6832741978545152951)
XLA Ops:
  0.6 78.1 %shard_map.104 = (f32[1571,1024]{1,0:T(8,128)}, f32[8,128]{1,0:T(8,128)}, bf16[64,360]{1,0:T(8,128)(2,1)}, bf16[4,2,4,4,8,2880]{5,4,3,2,1,0:T(8,128)(2,1)}) custom-call(bf16[64,2880]{1,0:T(8,128)(2,1)} %t_ref.1, bf16[8,2880]{1,0:T(8,128)(2,1)} %a_ref.1, s32[4,64]{1,0:T(4,128)} %bitcast.14, bf16[64,2880]{1,0:T(8,128)(2,1)} %bitcast.11, s32[1,1024]{1,0:T(1,128)} %bitcast.13, ...), custom_call_target="tpu_custom_call" | custom-call | tf_op jit(solution)/shard_map/pallas_call | solution.py:486
  78.7 6.5 %shard_map.105 = (f32[1571,1024]{1,0:T(8,128)}, bf16[64,360]{1,0:T(8,128)(2,1)}) custom-call(f32[1571,1024]{1,0:T(8,128)} %get-tuple-element.7.s_ref, f32[1,1024]{1,0:T(1,128)} %bitcast.12, bf16[64,360]{1,0:T(8,128)(2,1)} %get-tuple-element.9.e_ref), custom_call_target="tpu_custom_call" | custom-call | tf_op jit(solution)/shard_map/pallas_call | solution.py:534
